TPU v7x, 32 devices: a whole 2x2x4 slice. The times are simulated.
32 devices in a mesh: gx: 2 (over core), gy: 4 (over y, x), gz: 4 (over z).
Axes of the slice: x: 2, y: 2, z: 4, core: 2. Of those that a mesh axis runs over, the one named last changes fastest.
Arguments:
- quant_codes: int32 [64, 128, 512], P('gx', 'gy', 'gz'), may hold values from -1073741824 to 1073741824, as said below
- error_step: float32 [1], replicated, may hold values from 4e-09 to 1.5e-08
Outputs:
- decoded: float32 [64, 128, 512], P('gx', 'gy', 'gz')
Inputs may be any that keep to these rules, and one draw needn't show every extreme that they name: quant_codes are the third differences (along the three dimensions, with zeros before the grid's first cells) of a field of integers between -134217728 and 134217728.
All inputs are finite; a program needn't handle non-finite values.
Results may differ from a plain program's by a relative error of at most 0.00002.
Values sent between devices are 32-bit elements; how exact they have to be, the bound alone decides.
A program may use at most 64 MiB of HBM per device.

v0:
```python
import functools

import jax
import jax.numpy as jnp
from jax import lax
from jax.experimental import pallas as pl
from jax.experimental.pallas import tpu as pltpu
from jax.sharding import PartitionSpec as P

MESH = pl.DeviceIdType.MESH
I32 = jnp.int32
F32 = jnp.float32
SUB = 8
GRANT = 16 * 2**20
UNROLL = 4


def iota(shape, dim):
    return lax.broadcasted_iota(I32, shape, dim)


def turn(x, by, dim):
    n = x.shape[dim]
    by = by % n
    if by == 0:
        return x
    if dim == 1 and n % 128 != 0:
        return jnp.concatenate([x[:, n - by :], x[:, : n - by]], 1)
    return pltpu.roll(x, by, dim)


def lane_scan(x):
    n = x.shape[1]
    tri = (iota((n, n), 0) <= iota((n, n), 1)).astype(F32)
    one, big = tri.astype(jnp.bfloat16), (tri * 256.0).astype(jnp.bfloat16)

    def times(part, m):
        return jnp.dot(part.astype(F32).astype(jnp.bfloat16), m, preferred_element_type=F32)

    low = times(x & 255, one) + times((x >> 8) & 255, big)
    high = times((x >> 16) & 255, one) + times(x >> 24, big)
    return low.astype(I32) + (high.astype(I32) << 16)


def row_scan(x):
    rows, n = x.shape
    s = iota((SUB, n), 0)
    out, carry = [], None
    for b in range(rows // SUB):
        v = x[b * SUB : (b + 1) * SUB]
        for d in (1, 2, 4):
            v = v + jnp.where(s >= d, pltpu.roll(v, d, 0), 0)
        if carry is not None:
            v = v + carry
        carry = jnp.broadcast_to(v[SUB - 1 : SUB], (SUB, n))
        out.append(v)
    return jnp.concatenate(out, 0) if len(out) > 1 else out[0]


def exchange(
    mesh_sizes, q_hbm, v_ref, eh_ref,
    q, scan, xs, xup, xdn, ys, yup, hy, ydn, lines, cup, cx, cy,
    zs, zup, ds, zdn, rx, ry, ryt, ax, hxc, by, hyc, carry,
    load_sem, xss, xrs, yss, yrs, css, crs, zss, zrs, dss, drs, ready,
):
    nx, ny, nz = mesh_sizes
    ni, nj, nk = q.shape
    nb = nj // SUB
    nl = ni * nb
    X, Y, Z = (lax.axis_index(a) for a in ("gx", "gy", "gz"))
    place = {"gx": X, "gy": Y, "gz": Z}
    size = {"gx": nx, "gy": ny, "gz": nz}
    last_x, last_y, last_z = X == nx - 1, Y == ny - 1, Z == nz - 1

    load = pltpu.make_async_copy(q_hbm, q, load_sem)
    load.start()
    barrier = pltpu.get_barrier_semaphore()

    def greet(to, axis, sem):
        pl.semaphore_signal(sem, inc=1, device_id={axis: to}, device_id_type=MESH)

    @pl.when(Z > 0)
    def _():
        greet(Z - 1, "gz", barrier)

    @pl.when(Z < nz - 1)
    def _():
        greet(Z + 1, "gz", barrier)

    for dx in range(nx):
        for dy in range(ny):
            if dx or dy:
                pl.semaphore_signal(
                    barrier, inc=1, device_id_type=MESH,
                    device_id={"gx": lax.rem(X + dx, nx), "gy": lax.rem(Y + dy, ny)},
                )

    ends = []

    def hear(d):
        @pl.when(Z + d < nz)
        def _():
            pl.semaphore_wait(ready.at[d - 2], 1)

            if d < nz - 1:
                @pl.when(Z > 0)
                def _():
                    greet(Z - 1, "gz", ready.at[d - 1])

    def up(axis, src, slots, ssem, rsem, steps=None):
        for d in steps or range(1, size[axis]):
            def copy(d=d):
                return pltpu.make_async_remote_copy(
                    src_ref=src, dst_ref=slots.at[d - 1], send_sem=ssem.at[d - 1],
                    recv_sem=rsem.at[d - 1], device_id={axis: place[axis] + d},
                    device_id_type=MESH,
                )

            here = place[axis] + d < size[axis]

            @pl.when(here)
            def _():
                copy().start()

            ends.append((here, copy))

    def up_sum(axis, src, slots, ssem, rsem, total):
        total[...] = jnp.zeros_like(total)
        for d in range(1, size[axis]):
            @pl.when(place[axis] >= d)
            def _():
                pltpu.make_async_remote_copy(
                    src_ref=src, dst_ref=slots.at[d - 1], send_sem=ssem.at[d - 1],
                    recv_sem=rsem.at[d - 1], device_id={axis: place[axis]},
                    device_id_type=MESH,
                ).wait_recv()
                total[...] += slots[d - 1]

    def down_copy(axis, src, dst, n):
        return pltpu.make_async_remote_copy(
            src_ref=src, dst_ref=dst, send_sem=dss.at[n], recv_sem=drs.at[n],
            device_id={axis: place[axis] - 1}, device_id_type=MESH,
        )

    def down(axis, src, dst, n):
        here = place[axis] > 0

        @pl.when(here)
        def _():
            down_copy(axis, src, dst, n).start()

        ends.append((here, lambda: down_copy(axis, src, dst, n)))

    def down_wait(axis, src, dst, n):
        @pl.when(place[axis] < size[axis] - 1)
        def _():
            down_copy(axis, src, dst, n).wait_recv()

        @pl.when(place[axis] == size[axis] - 1)
        def _():
            dst[...] = jnp.zeros_like(dst)

    lanes = iota((SUB, nl), 1)
    subs = iota((SUB, nl), 0)

    load.wait()
    total = q[0]
    for i in range(1, ni):
        total = total + q[i]
    xs[...] = total
    for i in range(ni):
        ys[pl.ds(i, 1), :] = jnp.sum(q[i], axis=0, keepdims=True)
        hy[pl.ds(i, 1), :] = q[i, 0:1, :]
    sk = iota((SUB, nk), 0)
    lines[...] = jnp.where(
        sk == 0, jnp.sum(total, axis=0, keepdims=True),
        jnp.where(
            sk == 1, jnp.sum(q[0], axis=0, keepdims=True),
            jnp.where(sk == 2, total[0:1], 0),
        ),
    )
    beside_z = (Z > 0).astype(I32) + (Z < nz - 1).astype(I32)
    pl.semaphore_wait(barrier, nx * ny - 1 + beside_z)
    down("gy", hy, ydn, 1)
    up("gy", ys, yup, yss, yrs)

    corners = []
    for dx in range(-1, nx):
        for dy in range(-1, ny):
            if dx > 0 and dy > 0:
                slot = cup.at[(dx - 1) * (ny - 1) + dy - 1]
            elif dx == -1 and dy > 0:
                slot = cx.at[dy - 1]
            elif dx > 0 and dy == -1:
                slot = cy.at[dx - 1]
            else:
                continue
            corners.append((dx, dy, slot, len(corners)))

    def inside(x, y):
        return (x >= 0) & (x < nx) & (y >= 0) & (y < ny)

    def corner_copy(dx, dy, slot, n):
        return pltpu.make_async_remote_copy(
            src_ref=lines, dst_ref=slot, send_sem=css.at[n], recv_sem=crs.at[n],
            device_id={"gx": X + dx, "gy": Y + dy}, device_id_type=MESH,
        )

    for c in corners:
        here = inside(X + c[0], Y + c[1])

        @pl.when(here)
        def _(c=c):
            corner_copy(*c).start()

        ends.append((here, functools.partial(corner_copy, *c)))
    up("gx", xs, xup, xss, xrs)
    down("gx", q.at[0], xdn, 0)
    if nz > 2:
        @pl.when((Z > 0) & (Z < nz - 1))
        def _():
            greet(Z - 1, "gz", ready.at[0])

    step = 8

    def scan_block(g, _):
        rows = pl.ds(g * step, step)
        part = q[rows].reshape(step * nj, nk)
        scan[rows] = lane_scan(part).reshape(step, nj, nk)
        return 0

    lax.fori_loop(0, ni // step, scan_block, 0)

    block = lax.rem(lanes, nb)

    def j_scan(w):
        for d in (1, 2, 4):
            w = w + jnp.where(subs >= d, pltpu.roll(w, d, 0), 0)
        whole = jnp.broadcast_to(w[SUB - 1 : SUB], w.shape)
        for d in range(1, nb):
            w = w + jnp.where(block >= d, turn(whole, d, 1), 0)
        return w

    def i_scan(w):
        d = nb
        while d < nl:
            w = w + jnp.where(lanes >= d, turn(w, d, 1), 0)
            d *= 2
        return w

    a0 = jnp.zeros((SUB, nl), I32)
    b0 = jnp.zeros((SUB, nl), I32)
    for i in range(ni):
        for b in range(nb):
            rows = slice(b * SUB, (b + 1) * SUB)
            here = lanes == i * nb + b
            a0 = jnp.where(here, scan[i, rows, nk - 1 : nk], a0)
            b0 = jnp.where(here, q[i, rows, 0:1], b0)
    up_sum("gx", xs, xup, xss, xrs, rx)
    down_wait("gx", q.at[0], xdn, 0)
    rxv, hxv = rx[...], xdn[...]
    lx = lane_scan(jnp.concatenate([rxv, hxv], 0))
    a2 = jnp.zeros((SUB, nl), I32)
    b2 = jnp.zeros((SUB, nl), I32)
    for b in range(2 * nb):
        rows = slice(b * SUB, (b + 1) * SUB)
        a2 = jnp.where(lanes == b, lx[rows, nk - 1 : nk], a2)
        if b < nb:
            b2 = jnp.where(lanes == b, rxv[rows, 0:1], b2)
    a0 = i_scan(j_scan(a0 + jnp.where(lanes < nb, a2, 0)))
    b0 = i_scan(j_scan(b0 + jnp.where(lanes < nb, b2, 0)))
    a2 = j_scan(a2)
    for d in range(2, nz):
        @pl.when(Z > 0)
        def _(d=d):
            hear(d)

    ax[...] = row_scan(lx[:nj])
    hxc[...] = row_scan(lx[nj:])

    up_sum("gy", ys, yup, yss, yrs, ry)
    ryt[...] = jnp.zeros_like(ryt)

    def gather_lines(wanted):
        for c in corners:
            row = 0 if c[0] > 0 and c[1] > 0 else 1 if c[1] > 0 else 2
            if (row == 0) != wanted:
                continue

            @pl.when(inside(X - c[0], Y - c[1]))
            def _(c=c, row=row):
                corner_copy(*c).wait_recv()
                ryt[...] += jnp.where(sk == row, c[2][...], 0)

    upto = (iota((ni, nl), 1) // nb) >= iota((ni, nl), 0)

    def along(column, extra):
        return jnp.sum(jnp.where(upto, column, 0), axis=0, keepdims=True) + extra

    gather_lines(True)
    ds[...] = b0 + along(ry[:, 0:1], ryt[0:1, 0:1])
    down("gz", ds, zdn, 2)
    down_wait("gy", hy, ydn, 1)
    gather_lines(False)
    ryv, rytv = ry[...], ryt[...]
    ly = lane_scan(jnp.concatenate([ryv, ydn[...], rytv], 0))
    lyl, lyh, lyt = ly[:ni], ly[ni : 2 * ni], ly[2 * ni :]
    lyht = lyt[2:3]
    end = slice(nk - 1, nk)
    y_low = along(lyl[:, end], lyt[0:1, end])
    y_high = along(lyh[:, end], lyht[0:1, end])
    zs[0:SUB] = a0 + y_low
    zs[SUB : 2 * SUB] = a2 + jnp.where(lanes < nb, lyt[0:1, end], lyt[1:2, end])
    zs[2 * SUB :] = jnp.where(subs == 0, y_low, jnp.where(subs == 1, y_high, 0))
    up("gz", zs, zup, zss, zrs, [1])

    rows_i = iota((ni, nk), 0)
    by[...] = row_scan(lyl + jnp.where(rows_i == 0, lyt[0:1], 0))
    hyc[...] = row_scan(lyh + jnp.where(rows_i == 0, lyht[0:1], 0))
    jrow = iota((nj, nk), 0)
    klane = iota((nj, nk), 1)
    plane = ax[...]

    def field(i, before):
        inner = before + row_scan(scan[i])
        return inner, inner + plane + by[pl.ds(i, 1), :]

    def stencil(i, low, mid, high):
        down_j = jnp.where(jrow == 0, by[pl.ds(i, 1), :], turn(mid, 1, 0))
        edge_j = jnp.where(last_y, 0, mid + hyc[pl.ds(i, 1), :])
        up_j = jnp.where(jrow == nj - 1, edge_j, turn(mid, nj - 1, 0))
        down_k = jnp.where(klane == 0, 0, turn(mid, 1, 1))
        edge_k = jnp.where(last_z, 0, mid)
        up_k = jnp.where(klane == nk - 1, edge_k, turn(mid, nk - 1, 1))
        v_ref[i] = 6 * mid + (low + high) + (down_j + up_j) + (down_k + up_k)

    def sweep(i, state):
        low, mid, before = state
        inner, high = field(i + 1, before)
        stencil(i, low, mid, high)
        return mid, high, inner

    inner, mid = field(0, jnp.zeros((nj, nk), I32))
    state = (plane + lyt[0:1], mid, inner)
    many = (ni - 1) // UNROLL

    def sweeps(g, state):
        for u in range(UNROLL):
            state = sweep(g * UNROLL + u, state)
        return state

    state = lax.fori_loop(0, many, sweeps, state)
    for i in range(many * UNROLL, ni - 1):
        state = sweep(i, state)
    low, mid, _ = state
    stencil(ni - 1, low, mid, jnp.where(last_x, 0, mid + hxc[...] + lyt[1:2]))

    for d in range(2, nz):
        @pl.when(Z == 0)
        def _(d=d):
            hear(d)

        up("gz", zs, zup, zss, zrs, [d])

    up_sum("gz", zs, zup, zss, zrs, carry)
    down_wait("gz", ds, zdn, 2)
    D, xe = carry[0:SUB], carry[SUB : 2 * SUB]
    y_low, y_high = carry[2 * SUB : 2 * SUB + 1], carry[2 * SUB + 1 : 2 * SUB + 2]
    down_i = jnp.where(lanes < nb, xe, turn(D, nb, 1))
    edge_i = jnp.where(last_x, 0, D + turn(xe, nl - 2 * nb, 1))
    up_i = jnp.where(lanes >= nl - nb, edge_i, turn(D, nl - nb, 1))
    t = pltpu.roll(D, 1, 0)
    down_j = jnp.where(subs == 0, jnp.where(block == 0, y_low, turn(t, 1, 1)), t)
    t = pltpu.roll(D, SUB - 1, 0)
    edge_j = jnp.where(last_y, 0, D + y_high)
    up_j = jnp.where(
        subs == SUB - 1, jnp.where(block == nb - 1, edge_j, turn(t, nl - 1, 1)), t
    )
    eh_ref[0:SUB] = 8 * D + (down_i + up_i) + (down_j + up_j)
    eh_ref[SUB : 2 * SUB] = jnp.where(last_z, -D, zdn[...])

    for here, copy in ends:
        @pl.when(here)
        def _():
            copy().wait_send()


def finish(step_ref, v_ref, eh_ref, out_hbm, out, sems):
    ni, nj, nk = out.shape
    nb = nj // SUB
    scale = step_ref[0] * (1.0 / 12.0)
    at_end = iota((SUB, nk), 1) == nk - 1
    E, EH = eh_ref[0:SUB], eh_ref[0:SUB] + eh_ref[SUB : 2 * SUB]
    pieces = sems.shape[0]
    depth = ni // pieces
    copies = []
    for p in range(pieces):
        for i in range(p * depth, (p + 1) * depth):
            for b in range(nb):
                v = i * nb + b
                rows = slice(b * SUB, (b + 1) * SUB)
                carry = jnp.where(at_end, EH[:, v : v + 1], E[:, v : v + 1])
                out[i, rows, :] = (v_ref[i, rows, :] + carry).astype(F32) * scale
        part = pl.ds(p * depth, depth)
        copy = pltpu.make_async_copy(out.at[part], out_hbm.at[part], sems.at[p])
        copy.start()
        copies.append(copy)
    for copy in copies:
        copy.wait()


def solution(mesh):
    sizes = tuple(mesh.shape[a] for a in ("gx", "gy", "gz"))
    nx, ny, nz = sizes

    def on_device(quant_codes, error_step):
        ni, nj, nk = quant_codes.shape
        nl = ni * nj // SUB
        vm = lambda *shape: pltpu.VMEM(shape, I32)
        dma = lambda n: pltpu.SemaphoreType.DMA((n,))
        scratch = [
            vm(ni, nj, nk), vm(ni, nj, nk),
            vm(nj, nk), vm(nx - 1, nj, nk), vm(nj, nk),
            vm(ni, nk), vm(ny - 1, ni, nk), vm(ni, nk), vm(ni, nk),
            vm(SUB, nk), vm((nx - 1) * (ny - 1), SUB, nk),
            vm(ny - 1, SUB, nk), vm(nx - 1, SUB, nk),
            vm(3 * SUB, nl), vm(nz - 1, 3 * SUB, nl), vm(SUB, nl), vm(SUB, nl),
            vm(nj, nk), vm(ni, nk), vm(SUB, nk),
            vm(nj, nk), vm(nj, nk), vm(ni, nk), vm(ni, nk),
            vm(3 * SUB, nl),
            pltpu.SemaphoreType.DMA,
            dma(nx - 1), dma(nx - 1), dma(ny - 1), dma(ny - 1),
            dma(nx * ny - 1 + nx * ny), dma(nx * ny - 1 + nx * ny), dma(nz - 1), dma(nz - 1),
            dma(3), dma(3),
            pltpu.SemaphoreType.REGULAR((max(nz - 2, 1),)),
        ]
        any_space = pl.BlockSpec(memory_space=pl.ANY)
        hbm = pl.BlockSpec(memory_space=pltpu.HBM)
        vmem = pl.BlockSpec(memory_space=pltpu.VMEM)
        v, eh = pl.pallas_call(
            functools.partial(exchange, sizes),
            out_shape=(
                jax.ShapeDtypeStruct((ni, nj, nk), I32),
                jax.ShapeDtypeStruct((2 * SUB, nl), I32),
            ),
            in_specs=[hbm],
            out_specs=(vmem, vmem),
            scratch_shapes=scratch,
            compiler_params=pltpu.CompilerParams(
                collective_id=0, has_side_effects=True, vmem_limit_bytes=GRANT
            ),
            name="exchange",
        )(pltpu.with_memory_space_constraint(quant_codes, pltpu.HBM))
        return pl.pallas_call(
            finish,
            out_shape=jax.ShapeDtypeStruct((ni, nj, nk), F32),
            in_specs=[pl.BlockSpec(memory_space=pltpu.SMEM), vmem, vmem],
            out_specs=any_space,
            scratch_shapes=[pltpu.VMEM((ni, nj, nk), F32), dma(4)],
            compiler_params=pltpu.CompilerParams(vmem_limit_bytes=16 * 2**20),
            name="finish",
        )(error_step, v, eh)

    return jax.shard_map(
        on_device, mesh=mesh, in_specs=(P("gx", "gy", "gz"), P()),
        out_specs=P("gx", "gy", "gz"), check_vma=False,
    )
```

profile of v0, /device:TPU:0, one launch (start us, length us, event | category | flops | bytes accessed | tf_op | source)
XLA Modules:
  0.0 11.6 jit_solution(17103797599845037884)
XLA Ops:
  0.7 9.8 %exchange.1 = (s32[32,32,128]{2,1,0:T(8,128)S(1)}, s32[16,128]{1,0:T(8,128)S(1)}) custom-call(s32[32,32,128]{2,1,0:T(8,128)} %q_hbm.1), custom_call_target="tpu_custom_call" | custom-call | tf_op jit(solution)/shard_map/exchange/pallas_call | solution.py:440
  10.4 1.2 %finish.1 = f32[32,32,128]{2,1,0:T(8,128)} custom-call(f32[1]{0:T(128)S(6)} %copy.3.step_ref, s32[32,32,128]{2,1,0:T(8,128)S(1)} %get-tuple-element.7.v_ref, s32[16,128]{1,0:T(8,128)S(1)} %get-tuple-element.8.eh_ref), custom_call_target="tpu_custom_call" | custom-call | tf_op jit(solution)/shard_map/finish/pallas_call | solution.py:454
where the time goes:
time: 11.8 us; the launch traced here: 11.6 us
  Pallas kernels  10.9 us (92%)
  between operations  0.66 us (6%)
    pallas_call x1, Pallas kernels, on_device(): pl.pallas_call(functools.partial(exchange, sizes), out_shape=(jax.ShapeDt...  9.76 us
    pallas_call x1, Pallas kernels, on_device(): pl.pallas_call(finish, out_shape=jax.ShapeDtypeStruct((ni, nj, nk), F32),...  1.19 us

commit v1 on v0

--- a/solution.py
+++ b/solution.py
@@ -428,17 +428,26 @@
             vm(nj, nk), vm(ni, nk), vm(SUB, nk),
             vm(nj, nk), vm(nj, nk), vm(ni, nk), vm(ni, nk),
             vm(3 * SUB, nl),
+        ]
+        semaphores = [
             pltpu.SemaphoreType.DMA,
             dma(nx - 1), dma(nx - 1), dma(ny - 1), dma(ny - 1),
             dma(nx * ny - 1 + nx * ny), dma(nx * ny - 1 + nx * ny), dma(nz - 1), dma(nz - 1),
             dma(3), dma(3),
             pltpu.SemaphoreType.REGULAR((max(nz - 2, 1),)),
         ]
+
+        def scoped(*refs):
+            def body(*sems):
+                exchange(sizes, *refs, *sems)
+
+            pl.run_scoped(body, *semaphores)
+
         any_space = pl.BlockSpec(memory_space=pl.ANY)
         hbm = pl.BlockSpec(memory_space=pltpu.HBM)
         vmem = pl.BlockSpec(memory_space=pltpu.VMEM)
         v, eh = pl.pallas_call(
-            functools.partial(exchange, sizes),
+            scoped,
             out_shape=(
                 jax.ShapeDtypeStruct((ni, nj, nk), I32),
                 jax.ShapeDtypeStruct((2 * SUB, nl), I32),

time: 11.8 us -> 11.3 us (0.958)
  Pallas kernels: 10.9 us -> 10.5 us
    pallas_call x1, Pallas kernels: 9.76 us -> 9.28 us  [on_device(): pl.pallas_call(scoped, out_shape=(jax.ShapeDtypeStruct((ni, nj, nk), I32)...]
where the time goes in v1:
time: 11.3 us; the launch traced here: 11.1 us
  Pallas kernels  10.5 us (93%)
  between operations  0.66 us (6%)
    pallas_call x1, Pallas kernels, on_device(): pl.pallas_call(scoped, out_shape=(jax.ShapeDtypeStruct((ni, nj, nk), I32)...  9.28 us
    pallas_call x1, Pallas kernels, on_device(): pl.pallas_call(finish, out_shape=jax.ShapeDtypeStruct((ni, nj, nk), F32),...  1.19 us

profile of v1, /device:TPU:0, one launch (start us, length us, event | category | flops | bytes accessed | tf_op | source)
XLA Modules:
  0.0 11.1 jit_solution(15061009773161207909)
XLA Ops:
  0.7 9.3 %exchange.1 = (s32[32,32,128]{2,1,0:T(8,128)S(1)}, s32[16,128]{1,0:T(8,128)S(1)}) custom-call(s32[32,32,128]{2,1,0:T(8,128)} %refs_0_.1), custom_call_target="tpu_custom_call" | custom-call | tf_op jit(solution)/shard_map/exchange/pallas_call | solution.py:449
  9.9 1.2 %finish.1 = f32[32,32,128]{2,1,0:T(8,128)} custom-call(f32[1]{0:T(128)S(6)} %copy.3.step_ref, s32[32,32,128]{2,1,0:T(8,128)S(1)} %get-tuple-element.7.v_ref, s32[16,128]{1,0:T(8,128)S(1)} %get-tuple-element.8.eh_ref), custom_call_target="tpu_custom_call" | custom-call | tf_op jit(solution)/shard_map/finish/pallas_call | solution.py:463

commit v2 on v1

v2 whole, which is shorter than its diff:
```python
import functools

import jax
import jax.numpy as jnp
from jax import lax
from jax.experimental import pallas as pl
from jax.experimental.pallas import tpu as pltpu
from jax.sharding import PartitionSpec as P

MESH = pl.DeviceIdType.MESH
I32 = jnp.int32
F32 = jnp.float32
SUB = 8
GRANT = 16 * 2**20
UNROLL = 4
DEEP = 16


def iota(shape, dim):
    return lax.broadcasted_iota(I32, shape, dim)


def turn(x, by, dim):
    n = x.shape[dim]
    by = by % n
    if by == 0:
        return x
    if dim == 1 and n % 128 != 0:
        return jnp.concatenate([x[:, n - by :], x[:, : n - by]], 1)
    return pltpu.roll(x, by, dim)


def lane_scan(x):
    n = x.shape[1]
    tri = (iota((n, n), 0) <= iota((n, n), 1)).astype(F32)
    one, big = tri.astype(jnp.bfloat16), (tri * 256.0).astype(jnp.bfloat16)

    def times(part, m):
        return jnp.dot(part.astype(F32).astype(jnp.bfloat16), m, preferred_element_type=F32)

    low = times(x & 255, one) + times((x >> 8) & 255, big)
    high = times((x >> 16) & 255, one) + times(x >> 24, big)
    return low.astype(I32) + (high.astype(I32) << 16)


def row_scan(x):
    rows, n = x.shape
    s = iota((SUB, n), 0)
    out, carry = [], None
    for b in range(rows // SUB):
        v = x[b * SUB : (b + 1) * SUB]
        for d in (1, 2, 4):
            v = v + jnp.where(s >= d, pltpu.roll(v, d, 0), 0)
        if carry is not None:
            v = v + carry
        carry = jnp.broadcast_to(v[SUB - 1 : SUB], (SUB, n))
        out.append(v)
    return jnp.concatenate(out, 0) if len(out) > 1 else out[0]


def exchange(
    mesh_sizes, q_hbm, v_ref, eh_ref,
    q, scan, xs, xup, xdn, ys, yup, hy, ydn, pk, pkin, dgin,
    zs, zup, ds, zdn, ax, hxc, by, hyc,
    load_sem, xss, xrs, yss, yrs, pss, prs, gss, grs, zss, zrs, dss, drs, ready,
):
    nx, ny, nz = mesh_sizes
    ni, nj, nk = q.shape
    nb = nj // SUB
    nl = ni * nb
    X, Y, Z = (lax.axis_index(a) for a in ("gx", "gy", "gz"))
    place = {"gx": X, "gy": Y, "gz": Z}
    size = {"gx": nx, "gy": ny, "gz": nz}
    last_x, last_y, last_z = X == nx - 1, Y == ny - 1, Z == nz - 1
    plane_to, level_to = messages(nx, ny)

    load = pltpu.make_async_copy(q_hbm, q, load_sem)
    load.start()
    barrier = pltpu.get_barrier_semaphore()

    def greet(to, sem):
        pl.semaphore_signal(sem, inc=1, device_id=to, device_id_type=MESH)

    def inside(x, y, z=0):
        ok = (x >= 0) & (x < nx) & (y >= 0) & (y < ny)
        return ok if isinstance(z, int) else ok & (z >= 0) & (z < nz)

    for dx in range(nx):
        for dy in range(ny):
            if dx or dy:
                greet({"gx": lax.rem(X + dx, nx), "gy": lax.rem(Y + dy, ny)}, barrier)
    first_y = Y == 0
    for d in (-2, -1, 1):
        @pl.when((Z + d >= 0) & (Z + d < nz) & (first_y if d == -2 else True))
        def _(d=d):
            greet({"gz": Z + d}, barrier)

    for dx, dy in level_to:
        @pl.when(inside(X - dx, Y - dy, Z + 1))
        def _(dx=dx, dy=dy):
            greet({"gx": X - dx, "gy": Y - dy, "gz": Z + 1}, barrier)

    near = sum(((Z + d >= 0) & (Z + d < nz)).astype(I32) for d in (-1, 1))
    near = near + (first_y & (Z + 2 < nz)).astype(I32)
    above = jnp.where(Z > 0, (nx - X) * (ny - 1 - Y), 0)
    awaited = nx * ny - 1 + near + above

    def clear(here, slot):
        @pl.when(here)
        def _():
            slot[...] = jnp.zeros(slot.shape, I32)

    for n, (dx, dy) in enumerate(plane_to):
        clear(jnp.logical_not(inside(X - dx, Y - dy)), pkin.at[n])
    for n, (dx, dy) in enumerate(level_to):
        clear(jnp.logical_not(inside(X - dx, Y - dy, Z + 1)), dgin.at[n])
    for axis, slots, beyond in (("gx", xup, xdn), ("gy", yup, ydn), ("gz", zup, zdn)):
        for d in range(1, size[axis]):
            clear(place[axis] < d, slots.at[d - 1])
        clear(place[axis] == size[axis] - 1, beyond)

    ends = []

    def send(here, copy):
        @pl.when(here)
        def _():
            copy().start()

    def up_copy(axis, src, slots, ssem, rsem, d):
        return pltpu.make_async_remote_copy(
            src_ref=src, dst_ref=slots.at[d - 1], send_sem=ssem.at[d - 1],
            recv_sem=rsem.at[d - 1], device_id={axis: place[axis] + d},
            device_id_type=MESH,
        )

    def ups(axis, *refs):
        return [
            (place[axis] + d < size[axis], functools.partial(up_copy, axis, *refs, d))
            for d in range(size[axis] - 1, 0, -1)
        ]

    def up_wait(axis, *refs):
        for d in range(1, size[axis]):
            @pl.when(place[axis] >= d)
            def _(d=d):
                up_copy(axis, *refs, d).wait_recv()

    def down_copy(axis, src, dst, n):
        return pltpu.make_async_remote_copy(
            src_ref=src, dst_ref=dst, send_sem=dss.at[n], recv_sem=drs.at[n],
            device_id={axis: place[axis] - 1}, device_id_type=MESH,
        )

    def downs(axis, src, dst, n):
        return [(place[axis] > 0, functools.partial(down_copy, axis, src, dst, n))]

    def down_wait(axis, src, dst, n):
        @pl.when(place[axis] < size[axis] - 1)
        def _():
            down_copy(axis, src, dst, n).wait_recv()

    def plane_copy(n):
        return pltpu.make_async_remote_copy(
            src_ref=pk, dst_ref=pkin.at[n], send_sem=pss.at[n], recv_sem=prs.at[n],
            device_id={"gx": X + plane_to[n][0], "gy": Y + plane_to[n][1]},
            device_id_type=MESH,
        )

    def level_copy(n):
        return pltpu.make_async_remote_copy(
            src_ref=pk.at[0:SUB], dst_ref=dgin.at[n], send_sem=gss.at[n],
            recv_sem=grs.at[n], device_id_type=MESH,
            device_id={"gx": X + level_to[n][0], "gy": Y + level_to[n][1], "gz": Z - 1},
        )

    lanes = iota((SUB, nl), 1)
    subs = iota((SUB, nl), 0)
    sk = iota((SUB, nk), 0)
    block = lax.rem(lanes, nb)
    end = slice(nk - 1, nk)
    upto = (iota((ni, nl), 1) // nb) >= iota((ni, nl), 0)

    def along(column):
        return jnp.sum(jnp.where(upto, column, 0), axis=0, keepdims=True)

    def j_scan(w):
        for d in (1, 2, 4):
            w = w + jnp.where(subs >= d, pltpu.roll(w, d, 0), 0)
        whole = jnp.broadcast_to(w[SUB - 1 : SUB], w.shape)
        for d in range(1, nb):
            w = w + jnp.where(block >= d, turn(whole, d, 1), 0)
        return w

    def i_scan(w):
        d = nb
        while d < nl:
            w = w + jnp.where(lanes >= d, turn(w, d, 1), 0)
            d *= 2
        return w

    load.wait()
    total = q[0]
    for i in range(1, ni):
        total = total + q[i]
    xs[...] = total
    for i in range(ni):
        ys[pl.ds(i, 1), :] = jnp.sum(q[i], axis=0, keepdims=True)
        hy[pl.ds(i, 1), :] = q[i, 0:1, :]
    lines = jnp.where(
        sk == 0, jnp.sum(total, axis=0, keepdims=True),
        jnp.where(
            sk == 1, jnp.sum(q[0], axis=0, keepdims=True),
            jnp.where(sk == 2, total[0:1], 0),
        ),
    )
    ysv = ys[...]
    small = lane_scan(jnp.concatenate([ysv, hy[...], lines], 0))[:, end]
    ends_of = jnp.broadcast_to(small[2 * ni :], (SUB, nl))
    row = [
        along(small[:ni]), ends_of[0:1], along(ysv[:, 0:1]),
        jnp.broadcast_to(lines[0:1, 0:1], (1, nl)), along(small[ni : 2 * ni]),
        ends_of[2:3], ends_of[1:2],
    ]
    rows = jnp.zeros((SUB, nl), I32)
    for r, value in enumerate(row):
        rows = jnp.where(subs == r, value, rows)
    pk[0:SUB] = rows
    pk[SUB:] = lines

    outgoing = [
        (inside(X + dx, Y + dy), functools.partial(plane_copy, n))
        for n, (dx, dy) in enumerate(plane_to)
    ] + [
        (inside(X + dx, Y + dy, Z - 1), functools.partial(level_copy, n))
        for n, (dx, dy) in enumerate(level_to)
    ]
    outgoing += ups("gx", xs, xup, xss, xrs) + downs("gx", q.at[0], xdn, 0)
    outgoing += downs("gy", hy, ydn, 1) + ups("gy", ys, yup, yss, yrs)
    ends.extend(outgoing)
    relays = [
        (base, (Z > 0) & (Z + base < nz) & (first_y == (base == 2)))
        for base in (1, 2) if nz > base + 1
    ]

    def burst():
        pl.semaphore_wait(barrier, awaited)
        for here, copy in outgoing:
            send(here, copy)
        for base, here in relays:
            @pl.when(here)
            def _(base=base):
                greet({"gz": Z - 1}, ready.at[base - 1])

    @pl.when(jnp.logical_not(first_y))
    def _():
        burst()

    deep = min(DEEP, ni)

    def scan_block(g, _):
        part = q[pl.ds(g * deep, deep)].reshape(deep * nj, nk)
        scan[pl.ds(g * deep, deep)] = lane_scan(part).reshape(deep, nj, nk)
        return 0

    lax.fori_loop(0, ni // deep, scan_block, 0)

    a0 = jnp.zeros((SUB, nl), I32)
    b0 = jnp.zeros((SUB, nl), I32)
    for i in range(ni):
        for b in range(nb):
            rows_b = slice(b * SUB, (b + 1) * SUB)
            here = lanes == i * nb + b
            a0 = jnp.where(here, scan[i, rows_b, end], a0)
            b0 = jnp.where(here, q[i, rows_b, 0:1], b0)
    a0 = i_scan(j_scan(a0))
    b0 = i_scan(j_scan(b0))
    ds[...] = b0

    @pl.when(first_y)
    def _():
        burst()

    [(below, down_ds)] = downs("gz", ds, zdn, 2)
    ends.append((below, down_ds))
    send(below & (X == 0), down_ds)

    def hear(d, also):
        @pl.when((Z + d < nz) & also & (True if d > 2 else jnp.logical_not(first_y)))
        def _():
            pl.semaphore_wait(ready.at[d - 2], 1)

            if d < nz - 1:
                @pl.when(Z > 0)
                def _():
                    greet({"gz": Z - 1}, ready.at[d - 1])

    for d in range(2, nz):
        hear(d, Z > 0)

    up_wait("gx", xs, xup, xss, xrs)
    down_wait("gx", q.at[0], xdn, 0)
    rxv = xup[0]
    for d in range(1, nx - 1):
        rxv = rxv + xup[d]
    lx = lane_scan(jnp.concatenate([rxv, xdn[...]], 0))
    a2 = jnp.zeros((SUB, nl), I32)
    b2 = jnp.zeros((SUB, nl), I32)
    for b in range(2 * nb):
        rows_b = slice(b * SUB, (b + 1) * SUB)
        a2 = jnp.where(lanes == b, lx[rows_b, end], a2)
        if b < nb:
            b2 = jnp.where(lanes == b, rxv[rows_b, 0:1], b2)
    a2 = j_scan(a2)
    b2 = j_scan(b2)
    a0 = a0 + i_scan(jnp.where(lanes < nb, a2, 0))

    @pl.when(X > 0)
    def _():
        ds[...] += i_scan(jnp.where(lanes < nb, b2, 0))

    send(below & (X > 0), down_ds)
    ax[...] = row_scan(lx[:nj])
    hxc[...] = row_scan(lx[nj:])

    for n, (dx, dy) in enumerate(plane_to):
        @pl.when(inside(X - dx, Y - dy))
        def _(n=n):
            plane_copy(n).wait_recv()

    def gather(wanted, slots):
        found = [slots(n) for n, m in enumerate(plane_to) if wanted(*m)]
        return functools.reduce(jnp.add, found) if found else jnp.zeros((SUB, nk), I32)

    kinds = (
        (lambda dx, dy: dx == 0 and dy > 0, 0), (lambda dx, dy: dx > 0 and dy > 0, 1),
        (lambda dx, dy: dx == 0 and dy < 0, 4), (lambda dx, dy: dx > 0 and dy < 0, 5),
        (lambda dx, dy: dx < 0, 6),
    )
    low, corner, high, high_corner, before = (
        gather(wanted, lambda n: pkin[n, 0:SUB])[r : r + 1] for wanted, r in kinds
    )
    y_low, y_high = low + corner, high + high_corner
    zs[0:SUB] = a0 + y_low
    zs[SUB : 2 * SUB] = a2 + jnp.where(lanes < nb, corner, before)
    zs[2 * SUB :] = jnp.where(subs == 0, y_low, jnp.where(subs == 1, y_high, 0))
    z_refs = (zs, zup, zss, zrs)
    higher = ups("gz", *z_refs)
    ends.extend(higher)
    for here, copy in higher:
        send(here & (Z > 0), copy)
    for d, (here, copy) in enumerate(reversed(higher), 1):
        if d > 1:
            hear(d, Z == 0)
        send(here & (Z == 0), copy)

    up_wait("gy", ys, yup, yss, yrs)
    down_wait("gy", hy, ydn, 1)
    ryv = yup[0]
    for d in range(1, ny - 1):
        ryv = ryv + yup[d]
    tail = lambda n: pkin[n, SUB:]
    rytv = jnp.where(
        sk == 0, gather(kinds[1][0], tail),
        jnp.where(
            sk == 1, gather(kinds[4][0], tail),
            jnp.where(sk == 2, gather(kinds[3][0], tail), 0),
        ),
    )
    ly = lane_scan(jnp.concatenate([ryv, ydn[...], rytv], 0))
    lyl, lyh, lyt = ly[:ni], ly[ni : 2 * ni], ly[2 * ni :]
    rows_i = iota((ni, nk), 0)
    by[...] = row_scan(lyl + jnp.where(rows_i == 0, lyt[0:1], 0))
    hyc[...] = row_scan(lyh + jnp.where(rows_i == 0, lyt[2:3], 0))
    jrow = iota((nj, nk), 0)
    klane = iota((nj, nk), 1)
    plane = ax[...]

    def field(i, before):
        inner = before + row_scan(scan[i])
        return inner, inner + plane + by[pl.ds(i, 1), :]

    def stencil(i, low, mid, high):
        down_j = jnp.where(jrow == 0, by[pl.ds(i, 1), :], turn(mid, 1, 0))
        edge_j = jnp.where(last_y, 0, mid + hyc[pl.ds(i, 1), :])
        up_j = jnp.where(jrow == nj - 1, edge_j, turn(mid, nj - 1, 0))
        down_k = jnp.where(klane == 0, 0, turn(mid, 1, 1))
        edge_k = jnp.where(last_z, 0, mid)
        up_k = jnp.where(klane == nk - 1, edge_k, turn(mid, nk - 1, 1))
        v_ref[i] = 6 * mid + (low + high) + (down_j + up_j) + (down_k + up_k)

    def sweep(i, state):
        low, mid, before = state
        inner, high = field(i + 1, before)
        stencil(i, low, mid, high)
        return mid, high, inner

    inner, mid = field(0, jnp.zeros((nj, nk), I32))
    state = (plane + lyt[0:1], mid, inner)
    many = (ni - 1) // UNROLL

    def sweeps(g, state):
        for u in range(UNROLL):
            state = sweep(g * UNROLL + u, state)
        return state

    state = lax.fori_loop(0, many, sweeps, state)
    for i in range(many * UNROLL, ni - 1):
        state = sweep(i, state)
    low, mid, _ = state
    stencil(ni - 1, low, mid, jnp.where(last_x, 0, mid + hxc[...] + lyt[1:2]))

    for n, (dx, dy) in enumerate(level_to):
        @pl.when(inside(X - dx, Y - dy, Z + 1))
        def _(n=n):
            level_copy(n).wait_recv()

    down_wait("gz", ds, zdn, 2)
    up_wait("gz", *z_refs)
    beyond = zdn[...]
    for n, (dx, dy) in enumerate(level_to):
        r = 2 if dx == 0 else 3
        beyond = beyond + dgin[n, r : r + 1, :]
    carry = zup[0]
    for d in range(1, nz - 1):
        carry = carry + zup[d]
    D, xe = carry[0:SUB], carry[SUB : 2 * SUB]
    y_low, y_high = carry[2 * SUB : 2 * SUB + 1], carry[2 * SUB + 1 : 2 * SUB + 2]
    down_i = jnp.where(lanes < nb, xe, turn(D, nb, 1))
    edge_i = jnp.where(last_x, 0, D + turn(xe, nl - 2 * nb, 1))
    up_i = jnp.where(lanes >= nl - nb, edge_i, turn(D, nl - nb, 1))
    t = pltpu.roll(D, 1, 0)
    down_j = jnp.where(subs == 0, jnp.where(block == 0, y_low, turn(t, 1, 1)), t)
    t = pltpu.roll(D, SUB - 1, 0)
    edge_j = jnp.where(last_y, 0, D + y_high)
    up_j = jnp.where(
        subs == SUB - 1, jnp.where(block == nb - 1, edge_j, turn(t, nl - 1, 1)), t
    )
    eh_ref[0:SUB] = 8 * D + (down_i + up_i) + (down_j + up_j)
    eh_ref[SUB : 2 * SUB] = jnp.where(last_z, -D, beyond)

    for here, copy in ends:
        @pl.when(here)
        def _():
            copy().wait_send()


def messages(nx, ny):
    plane = [
        (dx, dy) for dy in range(ny - 1, 0, -1) for dx in range(-1, nx)
    ] + [(dx, -1) for dx in range(nx)]
    level = [(dx, dy) for dy in range(ny - 1, 0, -1) for dx in range(nx)]
    return plane, level


def finish(step_ref, v_ref, eh_ref, out_hbm, out, sems):
    ni, nj, nk = out.shape
    nb = nj // SUB
    scale = step_ref[0] * (1.0 / 12.0)
    at_end = iota((SUB, nk), 1) == nk - 1
    E, EH = eh_ref[0:SUB], eh_ref[0:SUB] + eh_ref[SUB : 2 * SUB]
    pieces = sems.shape[0]
    depth = ni // pieces
    copies = []
    for p in range(pieces):
        for i in range(p * depth, (p + 1) * depth):
            for b in range(nb):
                v = i * nb + b
                rows = slice(b * SUB, (b + 1) * SUB)
                carry = jnp.where(at_end, EH[:, v : v + 1], E[:, v : v + 1])
                out[i, rows, :] = (v_ref[i, rows, :] + carry).astype(F32) * scale
        part = pl.ds(p * depth, depth)
        copy = pltpu.make_async_copy(out.at[part], out_hbm.at[part], sems.at[p])
        copy.start()
        copies.append(copy)
    for copy in copies:
        copy.wait()


def solution(mesh):
    sizes = tuple(mesh.shape[a] for a in ("gx", "gy", "gz"))
    nx, ny, nz = sizes

    def on_device(quant_codes, error_step):
        ni, nj, nk = quant_codes.shape
        nl = ni * nj // SUB
        vm = lambda *shape: pltpu.VMEM(shape, I32)
        dma = lambda n: pltpu.SemaphoreType.DMA((n,))
        plane_to, level_to = messages(nx, ny)
        np_, ng = len(plane_to), len(level_to)
        scratch = [
            vm(ni, nj, nk), vm(ni, nj, nk),
            vm(nj, nk), vm(nx - 1, nj, nk), vm(nj, nk),
            vm(ni, nk), vm(ny - 1, ni, nk), vm(ni, nk), vm(ni, nk),
            vm(2 * SUB, nl), vm(np_, 2 * SUB, nl), vm(ng, SUB, nl),
            vm(3 * SUB, nl), vm(nz - 1, 3 * SUB, nl), vm(SUB, nl), vm(SUB, nl),
            vm(nj, nk), vm(nj, nk), vm(ni, nk), vm(ni, nk),
        ]
        semaphores = [
            pltpu.SemaphoreType.DMA,
            dma(nx - 1), dma(nx - 1), dma(ny - 1), dma(ny - 1),
            dma(np_), dma(np_), dma(ng), dma(ng), dma(nz - 1), dma(nz - 1),
            dma(3), dma(3),
            pltpu.SemaphoreType.REGULAR((max(nz - 2, 1),)),
        ]

        def scoped(*refs):
            def body(*sems):
                exchange(sizes, *refs, *sems)

            pl.run_scoped(body, *semaphores)

        any_space = pl.BlockSpec(memory_space=pl.ANY)
        hbm = pl.BlockSpec(memory_space=pltpu.HBM)
        vmem = pl.BlockSpec(memory_space=pltpu.VMEM)
        v, eh = pl.pallas_call(
            scoped,
            out_shape=(
                jax.ShapeDtypeStruct((ni, nj, nk), I32),
                jax.ShapeDtypeStruct((2 * SUB, nl), I32),
            ),
            in_specs=[hbm],
            out_specs=(vmem, vmem),
            scratch_shapes=scratch,
            compiler_params=pltpu.CompilerParams(
                collective_id=0, has_side_effects=True, vmem_limit_bytes=GRANT
            ),
            name="exchange",
        )(pltpu.with_memory_space_constraint(quant_codes, pltpu.HBM))
        return pl.pallas_call(
            finish,
            out_shape=jax.ShapeDtypeStruct((ni, nj, nk), F32),
            in_specs=[pl.BlockSpec(memory_space=pltpu.SMEM), vmem, vmem],
            out_specs=any_space,
            scratch_shapes=[pltpu.VMEM((ni, nj, nk), F32), dma(4)],
            compiler_params=pltpu.CompilerParams(vmem_limit_bytes=16 * 2**20),
            name="finish",
        )(error_step, v, eh)

    return jax.shard_map(
        on_device, mesh=mesh, in_specs=(P("gx", "gy", "gz"), P()),
        out_specs=P("gx", "gy", "gz"), check_vma=False,
    )
```

time: 11.3 us -> 10.4 us (0.920)
  the two profiles are of different devices: /device:TPU:0 before, /device:TPU:1 now
where the time goes in v2:
time: 10.4 us; the launch traced here: 10.2 us
  Pallas kernels  9.57 us (92%)
  between operations  0.66 us (6%)
    pallas_call x1, Pallas kernels, on_device(): pl.pallas_call(scoped, out_shape=(jax.ShapeDtypeStruct((ni, nj, nk), I32)...  8.38 us
    pallas_call x1, Pallas kernels, on_device(): pl.pallas_call(finish, out_shape=jax.ShapeDtypeStruct((ni, nj, nk), F32),...  1.19 us

profile of v2, /device:TPU:1, one launch (start us, length us, event | category | flops | bytes accessed | tf_op | source)
XLA Modules:
  0.0 10.2 jit_solution(5436014106073740891)
XLA Ops:
  0.7 8.4 %exchange.1 = (s32[32,32,128]{2,1,0:T(8,128)S(1)}, s32[16,128]{1,0:T(8,128)S(1)}) custom-call(s32[32,32,128]{2,1,0:T(8,128)} %refs_0_.1), custom_call_target="tpu_custom_call" | custom-call | tf_op jit(solution)/shard_map/exchange/pallas_call | solution.py:515
  9.0 1.2 %finish.1 = f32[32,32,128]{2,1,0:T(8,128)} custom-call(f32[1]{0:T(128)S(6)} %copy.3.step_ref, s32[32,32,128]{2,1,0:T(8,128)S(1)} %get-tuple-element.7.v_ref, s32[16,128]{1,0:T(8,128)S(1)} %get-tuple-element.8.eh_ref), custom_call_target="tpu_custom_call" | custom-call | tf_op jit(solution)/shard_map/finish/pallas_call | solution.py:529

commit v3 on v2

--- a/solution.py
+++ b/solution.py
@@ -14,6 +14,7 @@
 GRANT = 16 * 2**20
 UNROLL = 4
 DEEP = 16
+TURNS = 8
 
 
 def iota(shape, dim):
@@ -60,9 +61,9 @@
 
 def exchange(
     mesh_sizes, q_hbm, v_ref, eh_ref,
-    q, scan, xs, xup, xdn, ys, yup, hy, ydn, pk, pkin, dgin,
-    zs, zup, ds, zdn, ax, hxc, by, hyc,
-    load_sem, xss, xrs, yss, yrs, pss, prs, gss, grs, zss, zrs, dss, drs, ready,
+    q, scan, xs, xup, xdn, ys, yup, hy, ydn, pk, pkin, px, pxin, dgin,
+    zs, zup, ds, zdn, ax, hxc, by, hyc, tails,
+    load_sem, xss, xrs, yss, yrs, pss, prs, ass, ars, gss, grs, zss, zrs, dss, drs, ready,
 ):
     nx, ny, nz = mesh_sizes
     ni, nj, nk = q.shape
@@ -73,6 +74,7 @@
     size = {"gx": nx, "gy": ny, "gz": nz}
     last_x, last_y, last_z = X == nx - 1, Y == ny - 1, Z == nz - 1
     plane_to, level_to = messages(nx, ny)
+    beside = [-1, *range(1, nx)]
 
     load = pltpu.make_async_copy(q_hbm, q, load_sem)
     load.start()
@@ -102,7 +104,7 @@
 
     near = sum(((Z + d >= 0) & (Z + d < nz)).astype(I32) for d in (-1, 1))
     near = near + (first_y & (Z + 2 < nz)).astype(I32)
-    above = jnp.where(Z > 0, (nx - X) * (ny - 1 - Y), 0)
+    above = jnp.where(Z > 0, (nx - X) * (ny - Y) - 1, 0)
     awaited = nx * ny - 1 + near + above
 
     def clear(here, slot):
@@ -112,6 +114,8 @@
 
     for n, (dx, dy) in enumerate(plane_to):
         clear(jnp.logical_not(inside(X - dx, Y - dy)), pkin.at[n])
+    for n, dx in enumerate(beside):
+        clear(jnp.logical_not(inside(X - dx, Y)), pxin.at[n])
     for n, (dx, dy) in enumerate(level_to):
         clear(jnp.logical_not(inside(X - dx, Y - dy, Z + 1)), dgin.at[n])
     for axis, slots, beyond in (("gx", xup, xdn), ("gy", yup, ydn), ("gz", zup, zdn)):
@@ -119,12 +123,16 @@
             clear(place[axis] < d, slots.at[d - 1])
         clear(place[axis] == size[axis] - 1, beyond)
 
-    ends = []
-
     def send(here, copy):
         @pl.when(here)
         def _():
             copy().start()
+
+    def finish_sends(started):
+        for here, copy in started:
+            @pl.when(here)
+            def _(copy=copy):
+                copy().wait_send()
 
     def up_copy(axis, src, slots, ssem, rsem, d):
         return pltpu.make_async_remote_copy(
@@ -161,14 +169,23 @@
 
     def plane_copy(n):
         return pltpu.make_async_remote_copy(
-            src_ref=pk, dst_ref=pkin.at[n], send_sem=pss.at[n], recv_sem=prs.at[n],
+            src_ref=pk if plane_to[n][0] else pk.at[0:SUB],
+            dst_ref=pkin.at[n] if plane_to[n][0] else pkin.at[n, 0:SUB],
+            send_sem=pss.at[n], recv_sem=prs.at[n],
             device_id={"gx": X + plane_to[n][0], "gy": Y + plane_to[n][1]},
             device_id_type=MESH,
         )
 
+    def beside_copy(n):
+        return pltpu.make_async_remote_copy(
+            src_ref=px, dst_ref=pxin.at[n], send_sem=ass.at[n], recv_sem=ars.at[n],
+            device_id={"gx": X + beside[n]}, device_id_type=MESH,
+        )
+
     def level_copy(n):
         return pltpu.make_async_remote_copy(
-            src_ref=pk.at[0:SUB], dst_ref=dgin.at[n], send_sem=gss.at[n],
+            src_ref=pk.at[0:SUB] if level_to[n][1] else px.at[SUB : 2 * SUB],
+            dst_ref=dgin.at[n], send_sem=gss.at[n],
             recv_sem=grs.at[n], device_id_type=MESH,
             device_id={"gx": X + level_to[n][0], "gy": Y + level_to[n][1], "gz": Z - 1},
         )
@@ -177,6 +194,8 @@
     subs = iota((SUB, nl), 0)
     sk = iota((SUB, nk), 0)
     block = lax.rem(lanes, nb)
+    half = nl // 2
+    moved = (subs > 1) & (subs < 4) & (lax.rem(lanes, 2 * nb) >= nb)
     end = slice(nk - 1, nk)
     upto = (iota((ni, nl), 1) // nb) >= iota((ni, nl), 0)
 
@@ -189,6 +208,12 @@
         whole = jnp.broadcast_to(w[SUB - 1 : SUB], w.shape)
         for d in range(1, nb):
             w = w + jnp.where(block >= d, turn(whole, d, 1), 0)
+        return w
+
+    def packed(column):
+        w = jnp.zeros((SUB, nl), I32)
+        for b in range(nb):
+            w = jnp.where(block == b, column[b * SUB : (b + 1) * SUB], w)
         return w
 
     def i_scan(w):
@@ -214,8 +239,8 @@
         ),
     )
     ysv = ys[...]
-    small = lane_scan(jnp.concatenate([ysv, hy[...], lines], 0))[:, end]
-    ends_of = jnp.broadcast_to(small[2 * ni :], (SUB, nl))
+    small = lane_scan(jnp.concatenate([ysv, hy[...], lines, total, q[0]], 0))[:, end]
+    ends_of = jnp.broadcast_to(small[2 * ni : 2 * ni + SUB], (SUB, nl))
     row = [
         along(small[:ni]), ends_of[0:1], along(ysv[:, 0:1]),
         jnp.broadcast_to(lines[0:1, 0:1], (1, nl)), along(small[ni : 2 * ni]),
@@ -234,23 +259,29 @@
         (inside(X + dx, Y + dy, Z - 1), functools.partial(level_copy, n))
         for n, (dx, dy) in enumerate(level_to)
     ]
+    outgoing += [
+        (inside(X + dx, Y), functools.partial(beside_copy, n)) for n, dx in enumerate(beside)
+    ]
     outgoing += ups("gx", xs, xup, xss, xrs) + downs("gx", q.at[0], xdn, 0)
     outgoing += downs("gy", hy, ydn, 1) + ups("gy", ys, yup, yss, yrs)
-    ends.extend(outgoing)
     relays = [
         (base, (Z > 0) & (Z + base < nz) & (first_y == (base == 2)))
         for base in (1, 2) if nz > base + 1
     ]
 
-    def burst():
+    def burst(before=()):
         pl.semaphore_wait(barrier, awaited)
-        for here, copy in outgoing:
+        for here, copy in [*before, *outgoing]:
             send(here, copy)
         for base, here in relays:
             @pl.when(here)
             def _(base=base):
                 greet({"gz": Z - 1}, ready.at[base - 1])
 
+    first = 2 * ni + SUB
+    px[0:SUB] = j_scan(packed(small[first : first + nj]))
+    px[SUB : 2 * SUB] = j_scan(packed(total[:, 0:1]))
+    px[2 * SUB :] = j_scan(packed(small[first + nj :]))
     @pl.when(jnp.logical_not(first_y))
     def _():
         burst()
@@ -264,25 +295,23 @@
 
     lax.fori_loop(0, ni // deep, scan_block, 0)
 
-    a0 = jnp.zeros((SUB, nl), I32)
-    b0 = jnp.zeros((SUB, nl), I32)
-    for i in range(ni):
-        for b in range(nb):
-            rows_b = slice(b * SUB, (b + 1) * SUB)
-            here = lanes == i * nb + b
-            a0 = jnp.where(here, scan[i, rows_b, end], a0)
-            b0 = jnp.where(here, q[i, rows_b, 0:1], b0)
-    a0 = i_scan(j_scan(a0))
-    b0 = i_scan(j_scan(b0))
-    ds[...] = b0
+    def columns(source, column):
+        w = jnp.zeros((SUB, nl), I32)
+        for i in range(ni):
+            for b in range(nb):
+                part = source[i, b * SUB : (b + 1) * SUB, column]
+                w = jnp.where(lanes == i * nb + b, part, w)
+        return i_scan(j_scan(w))
+
+    ds[...] = columns(q, slice(0, 1))
+    [(below, down_ds)] = downs("gz", ds, zdn, 2)
 
     @pl.when(first_y)
     def _():
-        burst()
-
-    [(below, down_ds)] = downs("gz", ds, zdn, 2)
-    ends.append((below, down_ds))
-    send(below & (X == 0), down_ds)
+        burst([(below, down_ds)])
+
+    send(below & jnp.logical_not(first_y), down_ds)
+    a0 = columns(scan, end)
 
     def hear(d, also):
         @pl.when((Z + d < nz) & also & (True if d > 2 else jnp.logical_not(first_y)))
@@ -297,30 +326,69 @@
     for d in range(2, nz):
         hear(d, Z > 0)
 
+    for n, dx in enumerate(beside):
+        @pl.when(inside(X - dx, Y))
+        def _(n=n):
+            beside_copy(n).wait_recv()
+
+    xa = pxin[1, 0:SUB]
+    for n in range(2, nx):
+        xa = xa + pxin[n, 0:SUB]
+    a0 = a0 + xa
+    xd = pxin[0, 2 * SUB :]
     up_wait("gx", xs, xup, xss, xrs)
     down_wait("gx", q.at[0], xdn, 0)
     rxv = xup[0]
     for d in range(1, nx - 1):
         rxv = rxv + xup[d]
     lx = lane_scan(jnp.concatenate([rxv, xdn[...]], 0))
-    a2 = jnp.zeros((SUB, nl), I32)
-    b2 = jnp.zeros((SUB, nl), I32)
-    for b in range(2 * nb):
-        rows_b = slice(b * SUB, (b + 1) * SUB)
-        a2 = jnp.where(lanes == b, lx[rows_b, end], a2)
-        if b < nb:
-            b2 = jnp.where(lanes == b, rxv[rows_b, 0:1], b2)
-    a2 = j_scan(a2)
-    b2 = j_scan(b2)
-    a0 = a0 + i_scan(jnp.where(lanes < nb, a2, 0))
-
-    @pl.when(X > 0)
-    def _():
-        ds[...] += i_scan(jnp.where(lanes < nb, b2, 0))
-
-    send(below & (X > 0), down_ds)
     ax[...] = row_scan(lx[:nj])
     hxc[...] = row_scan(lx[nj:])
+
+    def sweep_all():
+        jrow = iota((nj, nk), 0)
+        klane = iota((nj, nk), 1)
+        plane = ax[...]
+
+        def field(i, before):
+            inner = before + row_scan(scan[i])
+            return inner, inner + plane + by[pl.ds(i, 1), :]
+
+        def stencil(i, low, mid, high):
+            down_j = jnp.where(jrow == 0, by[pl.ds(i, 1), :], turn(mid, 1, 0))
+            edge_j = jnp.where(last_y, 0, mid)
+            up_j = jnp.where(jrow == nj - 1, edge_j, turn(mid, nj - 1, 0))
+            down_k = jnp.where(klane == 0, 0, turn(mid, 1, 1))
+            edge_k = jnp.where(last_z, 0, mid)
+            up_k = jnp.where(klane == nk - 1, edge_k, turn(mid, nk - 1, 1))
+            v_ref[i] = 6 * mid + (low + high) + (down_j + up_j) + (down_k + up_k)
+
+        def sweep(i, state):
+            low, mid, before = state
+            inner, high = field(i + 1, before)
+            stencil(i, low, mid, high)
+            return mid, high, inner
+
+        inner, mid = field(0, jnp.zeros((nj, nk), I32))
+        state = (plane + tails[0:1], mid, inner)
+        many = (ni - 1) // UNROLL
+
+        def sweeps(g, state):
+            for u in range(UNROLL):
+                state = sweep(g * UNROLL + u, state)
+            return state
+
+        state = lax.fori_loop(0, many, sweeps, state)
+        for i in range(many * UNROLL, ni - 1):
+            state = sweep(i, state)
+        low, mid, _ = state
+        stencil(ni - 1, low, mid, jnp.where(last_x, 0, mid + hxc[...] + tails[1:2]))
+
+    @pl.when(first_y)
+    def _():
+        tails[...] = jnp.zeros_like(tails)
+        by[...] = jnp.zeros_like(by)
+        sweep_all()
 
     for n, (dx, dy) in enumerate(plane_to):
         @pl.when(inside(X - dx, Y - dy))
@@ -340,18 +408,24 @@
         gather(wanted, lambda n: pkin[n, 0:SUB])[r : r + 1] for wanted, r in kinds
     )
     y_low, y_high = low + corner, high + high_corner
+    front, back = xa + corner, xd + before
     zs[0:SUB] = a0 + y_low
-    zs[SUB : 2 * SUB] = a2 + jnp.where(lanes < nb, corner, before)
-    zs[2 * SUB :] = jnp.where(subs == 0, y_low, jnp.where(subs == 1, y_high, 0))
+    zs[SUB:] = jnp.where(
+        subs == 0, y_low,
+        jnp.where(
+            subs == 1, y_high,
+            jnp.where(
+                lanes < half, jnp.where(moved, pltpu.roll(front, 2, 0), front),
+                jnp.where(moved, pltpu.roll(back, 2, 0), back),
+            ),
+        ),
+    )
     z_refs = (zs, zup, zss, zrs)
     higher = ups("gz", *z_refs)
-    ends.extend(higher)
+    for d in range(2, nz):
+        hear(d, Z == 0)
     for here, copy in higher:
-        send(here & (Z > 0), copy)
-    for d, (here, copy) in enumerate(reversed(higher), 1):
-        if d > 1:
-            hear(d, Z == 0)
-        send(here & (Z == 0), copy)
+        send(here, copy)
 
     up_wait("gy", ys, yup, yss, yrs)
     down_wait("gy", hy, ydn, 1)
@@ -369,46 +443,19 @@
     ly = lane_scan(jnp.concatenate([ryv, ydn[...], rytv], 0))
     lyl, lyh, lyt = ly[:ni], ly[ni : 2 * ni], ly[2 * ni :]
     rows_i = iota((ni, nk), 0)
-    by[...] = row_scan(lyl + jnp.where(rows_i == 0, lyt[0:1], 0))
     hyc[...] = row_scan(lyh + jnp.where(rows_i == 0, lyt[2:3], 0))
-    jrow = iota((nj, nk), 0)
-    klane = iota((nj, nk), 1)
-    plane = ax[...]
-
-    def field(i, before):
-        inner = before + row_scan(scan[i])
-        return inner, inner + plane + by[pl.ds(i, 1), :]
-
-    def stencil(i, low, mid, high):
-        down_j = jnp.where(jrow == 0, by[pl.ds(i, 1), :], turn(mid, 1, 0))
-        edge_j = jnp.where(last_y, 0, mid + hyc[pl.ds(i, 1), :])
-        up_j = jnp.where(jrow == nj - 1, edge_j, turn(mid, nj - 1, 0))
-        down_k = jnp.where(klane == 0, 0, turn(mid, 1, 1))
-        edge_k = jnp.where(last_z, 0, mid)
-        up_k = jnp.where(klane == nk - 1, edge_k, turn(mid, nk - 1, 1))
-        v_ref[i] = 6 * mid + (low + high) + (down_j + up_j) + (down_k + up_k)
-
-    def sweep(i, state):
-        low, mid, before = state
-        inner, high = field(i + 1, before)
-        stencil(i, low, mid, high)
-        return mid, high, inner
-
-    inner, mid = field(0, jnp.zeros((nj, nk), I32))
-    state = (plane + lyt[0:1], mid, inner)
-    many = (ni - 1) // UNROLL
-
-    def sweeps(g, state):
-        for u in range(UNROLL):
-            state = sweep(g * UNROLL + u, state)
-        return state
-
-    state = lax.fori_loop(0, many, sweeps, state)
-    for i in range(many * UNROLL, ni - 1):
-        state = sweep(i, state)
-    low, mid, _ = state
-    stencil(ni - 1, low, mid, jnp.where(last_x, 0, mid + hxc[...] + lyt[1:2]))
-
+
+    @pl.when(jnp.logical_not(first_y))
+    def _():
+        tails[...] = lyt
+        by[...] = row_scan(lyl + jnp.where(rows_i == 0, lyt[0:1], 0))
+        sweep_all()
+
+    for i in range(ni):
+        beyond_j = jnp.where(sk == SUB - 1, hyc[pl.ds(i, 1), :], 0)
+        v_ref[i, nj - SUB : nj, :] += jnp.where(last_y, 0, beyond_j)
+
+    finish_sends([*outgoing, (below, down_ds)])
     for n, (dx, dy) in enumerate(level_to):
         @pl.when(inside(X - dx, Y - dy, Z + 1))
         def _(n=n):
@@ -419,36 +466,46 @@
     beyond = zdn[...]
     for n, (dx, dy) in enumerate(level_to):
         r = 2 if dx == 0 else 3
-        beyond = beyond + dgin[n, r : r + 1, :]
+        beyond = beyond + (dgin[n, r : r + 1, :] if dy else dgin[n])
     carry = zup[0]
     for d in range(1, nz - 1):
         carry = carry + zup[d]
-    D, xe = carry[0:SUB], carry[SUB : 2 * SUB]
-    y_low, y_high = carry[2 * SUB : 2 * SUB + 1], carry[2 * SUB + 1 : 2 * SUB + 2]
-    down_i = jnp.where(lanes < nb, xe, turn(D, nb, 1))
-    edge_i = jnp.where(last_x, 0, D + turn(xe, nl - 2 * nb, 1))
-    up_i = jnp.where(lanes >= nl - nb, edge_i, turn(D, nl - nb, 1))
-    t = pltpu.roll(D, 1, 0)
-    down_j = jnp.where(subs == 0, jnp.where(block == 0, y_low, turn(t, 1, 1)), t)
-    t = pltpu.roll(D, SUB - 1, 0)
-    edge_j = jnp.where(last_y, 0, D + y_high)
-    up_j = jnp.where(
-        subs == SUB - 1, jnp.where(block == nb - 1, edge_j, turn(t, nl - 1, 1)), t
-    )
-    eh_ref[0:SUB] = 8 * D + (down_i + up_i) + (down_j + up_j)
-    eh_ref[SUB : 2 * SUB] = jnp.where(last_z, -D, beyond)
-
-    for here, copy in ends:
-        @pl.when(here)
-        def _():
-            copy().wait_send()
+    D, edges = carry[0:SUB], carry[SUB:]
+    y_low = jnp.broadcast_to(edges[0:1], D.shape)
+    y_high = jnp.where(last_y, 0, jnp.broadcast_to(edges[1:2], D.shape))
+    lifted = pltpu.roll(edges, SUB - 2, 0)
+    prior, after = pltpu.roll(D, 1, 0), pltpu.roll(D, SUB - 1, 0)
+
+    def finals(by):
+        at = lax.rem(lanes + (nl - by), nl)
+        moved_to = lambda w, d: turn(w, d + by, 1)
+        here = moved_to(D, 0)
+        front = jnp.where(subs < 2, moved_to(lifted, nl - nb), moved_to(edges, 0))
+        back = jnp.where(subs < 2, moved_to(lifted, 0), moved_to(edges, nb))
+        down_i = jnp.where(at < nb, front, moved_to(D, nb))
+        edge_i = jnp.where(last_x, 0, here + back)
+        up_i = jnp.where(at >= nl - nb, edge_i, moved_to(D, nl - nb))
+        edge_j = jnp.where(block == 0, moved_to(y_low, 0), moved_to(prior, 1))
+        down_j = jnp.where(subs == 0, edge_j, moved_to(prior, 0))
+        edge_j = jnp.where(last_y, 0, here + moved_to(y_high, 0))
+        edge_j = jnp.where(block == nb - 1, edge_j, moved_to(after, nl - 1))
+        up_j = jnp.where(subs == SUB - 1, edge_j, moved_to(after, 0))
+        E = 8 * here + (down_i + up_i) + (down_j + up_j)
+        return E, E + jnp.where(last_z, -here, moved_to(beyond, 0))
+
+    E, EH = finals(0)
+    E_half, EH_half = finals(half)
+    eh_ref[0:SUB] = jnp.where(lanes < half, E, EH_half)
+    eh_ref[SUB : 2 * SUB] = jnp.where(lanes < half, E_half, EH)
+
+    finish_sends(higher)
 
 
 def messages(nx, ny):
-    plane = [
+    plane = [(dx, -1) for dx in range(nx)] + [
         (dx, dy) for dy in range(ny - 1, 0, -1) for dx in range(-1, nx)
-    ] + [(dx, -1) for dx in range(nx)]
-    level = [(dx, dy) for dy in range(ny - 1, 0, -1) for dx in range(nx)]
+    ]
+    level = [(dx, dy) for dy in range(ny - 1, -1, -1) for dx in range(nx) if dx or dy]
     return plane, level
 
 
@@ -456,22 +513,29 @@
     ni, nj, nk = out.shape
     nb = nj // SUB
     scale = step_ref[0] * (1.0 / 12.0)
-    at_end = iota((SUB, nk), 1) == nk - 1
-    E, EH = eh_ref[0:SUB], eh_ref[0:SUB] + eh_ref[SUB : 2 * SUB]
-    pieces = sems.shape[0]
-    depth = ni // pieces
+    half = ni * nb // 2
+    base = jnp.where(iota((SUB, nk), 1) == nk - 1, half, 0)
+    halves = eh_ref[0:SUB], eh_ref[SUB : 2 * SUB]
+    steps = sems.shape[0] // 2
+    depth = ni // 2 // steps
+    turned = [[turn(w, half * 2 - c, 1) for c in range(TURNS)] for w in halves]
     copies = []
-    for p in range(pieces):
+    for p in range(steps):
         for i in range(p * depth, (p + 1) * depth):
             for b in range(nb):
                 v = i * nb + b
+                c = v % TURNS
                 rows = slice(b * SUB, (b + 1) * SUB)
-                carry = jnp.where(at_end, EH[:, v : v + 1], E[:, v : v + 1])
-                out[i, rows, :] = (v_ref[i, rows, :] + carry).astype(F32) * scale
-        part = pl.ds(p * depth, depth)
-        copy = pltpu.make_async_copy(out.at[part], out_hbm.at[part], sems.at[p])
-        copy.start()
-        copies.append(copy)
+                for at, source in ((i, turned[0][c]), (i + ni // 2, turned[1][c])):
+                    carry = jnp.take_along_axis(
+                        source, base + (v - c), 1, mode="promise_in_bounds"
+                    )
+                    out[at, rows, :] = (v_ref[at, rows, :] + carry).astype(F32) * scale
+        for h in range(2):
+            part = pl.ds(h * (ni // 2) + p * depth, depth)
+            copy = pltpu.make_async_copy(out.at[part], out_hbm.at[part], sems.at[2 * p + h])
+            copy.start()
+            copies.append(copy)
     for copy in copies:
         copy.wait()
 
@@ -491,14 +555,15 @@
             vm(ni, nj, nk), vm(ni, nj, nk),
             vm(nj, nk), vm(nx - 1, nj, nk), vm(nj, nk),
             vm(ni, nk), vm(ny - 1, ni, nk), vm(ni, nk), vm(ni, nk),
-            vm(2 * SUB, nl), vm(np_, 2 * SUB, nl), vm(ng, SUB, nl),
-            vm(3 * SUB, nl), vm(nz - 1, 3 * SUB, nl), vm(SUB, nl), vm(SUB, nl),
-            vm(nj, nk), vm(nj, nk), vm(ni, nk), vm(ni, nk),
+            vm(2 * SUB, nl), vm(np_, 2 * SUB, nl), vm(3 * SUB, nl), vm(nx, 3 * SUB, nl),
+            vm(ng, SUB, nl),
+            vm(2 * SUB, nl), vm(nz - 1, 2 * SUB, nl), vm(SUB, nl), vm(SUB, nl),
+            vm(nj, nk), vm(nj, nk), vm(ni, nk), vm(ni, nk), vm(SUB, nk),
         ]
         semaphores = [
             pltpu.SemaphoreType.DMA,
             dma(nx - 1), dma(nx - 1), dma(ny - 1), dma(ny - 1),
-            dma(np_), dma(np_), dma(ng), dma(ng), dma(nz - 1), dma(nz - 1),
+            dma(np_), dma(np_), dma(nx), dma(nx), dma(ng), dma(ng), dma(nz - 1), dma(nz - 1),
             dma(3), dma(3),
             pltpu.SemaphoreType.REGULAR((max(nz - 2, 1),)),
         ]
@@ -531,7 +596,7 @@
             out_shape=jax.ShapeDtypeStruct((ni, nj, nk), F32),
             in_specs=[pl.BlockSpec(memory_space=pltpu.SMEM), vmem, vmem],
             out_specs=any_space,
-            scratch_shapes=[pltpu.VMEM((ni, nj, nk), F32), dma(4)],
+            scratch_shapes=[pltpu.VMEM((ni, nj, nk), F32), dma(8)],
             compiler_params=pltpu.CompilerParams(vmem_limit_bytes=16 * 2**20),
             name="finish",
         )(error_step, v, eh)

time: 10.4 us -> 9.62 us (0.925)
  the two profiles are of different devices: /device:TPU:1 before, /device:TPU:0 now
where the time goes in v3:
time: 9.62 us; the launch traced here: 9.45 us
  Pallas kernels  8.8 us (91%)
  between operations  0.65 us (7%)
    pallas_call x1, Pallas kernels, on_device(): pl.pallas_call(scoped, out_shape=(jax.ShapeDtypeStruct((ni, nj, nk), I32)...  7.78 us
    pallas_call x1, Pallas kernels, on_device(): pl.pallas_call(finish, out_shape=jax.ShapeDtypeStruct((ni, nj, nk), F32),...  1.02 us

profile of v3, /device:TPU:0, one launch (start us, length us, event | category | flops | bytes accessed | tf_op | source)
XLA Modules:
  0.0 9.5 jit_solution(1942675669084391962)
XLA Ops:
  0.7 7.8 %exchange.1 = (s32[32,32,128]{2,1,0:T(8,128)S(1)}, s32[16,128]{1,0:T(8,128)S(1)}) custom-call(s32[32,32,128]{2,1,0:T(8,128)} %refs_0_.1), custom_call_target="tpu_custom_call" | custom-call | tf_op jit(solution)/shard_map/exchange/pallas_call | solution.py:580
  8.4 1.0 %finish.1 = f32[32,32,128]{2,1,0:T(8,128)} custom-call(f32[1]{0:T(128)S(6)} %copy.3.step_ref, s32[32,32,128]{2,1,0:T(8,128)S(1)} %get-tuple-element.7.v_ref, s32[16,128]{1,0:T(8,128)S(1)} %get-tuple-element.8.eh_ref), custom_call_target="tpu_custom_call" | custom-call | tf_op jit(solution)/shard_map/finish/pallas_call | solution.py:594

commit v4 on v3

--- a/solution.py
+++ b/solution.py
@@ -62,8 +62,8 @@
 def exchange(
     mesh_sizes, q_hbm, v_ref, eh_ref,
     q, scan, xs, xup, xdn, ys, yup, hy, ydn, pk, pkin, px, pxin, dgin,
-    zs, zup, ds, zdn, ax, hxc, by, hyc, tails,
-    load_sem, xss, xrs, yss, yrs, pss, prs, ass, ars, gss, grs, zss, zrs, dss, drs, ready,
+    zs, zup, zr, zrin, ds, zdn, ax, hxc, by, hyc, tails,
+    load_sem, xss, xrs, yss, yrs, pss, prs, ass, ars, gss, grs, zss, zrs, rss, rrs, dss, drs, ready,
 ):
     nx, ny, nz = mesh_sizes
     ni, nj, nk = q.shape
@@ -118,10 +118,11 @@
         clear(jnp.logical_not(inside(X - dx, Y)), pxin.at[n])
     for n, (dx, dy) in enumerate(level_to):
         clear(jnp.logical_not(inside(X - dx, Y - dy, Z + 1)), dgin.at[n])
-    for axis, slots, beyond in (("gx", xup, xdn), ("gy", yup, ydn), ("gz", zup, zdn)):
+    for axis, slots, beyond in (("gx", xup, xdn), ("gy", yup, ydn), ("gz", zup, zdn), ("gz", zrin, None)):
         for d in range(1, size[axis]):
             clear(place[axis] < d, slots.at[d - 1])
-        clear(place[axis] == size[axis] - 1, beyond)
+        if beyond is not None:
+            clear(place[axis] == size[axis] - 1, beyond)
 
     def send(here, copy):
         @pl.when(here)
@@ -195,7 +196,17 @@
     sk = iota((SUB, nk), 0)
     block = lax.rem(lanes, nb)
     half = nl // 2
-    moved = (subs > 1) & (subs < 4) & (lax.rem(lanes, 2 * nb) >= nb)
+    starts = (0, nj, 2 * nj, 2 * nj + ni, 2 * (nj + ni))
+    lane = iota((1, nl), 1)
+
+    def within(k):
+        return (lane >= starts[k]) & (lane < starts[k + 1])
+
+    def in_order(column, k):
+        n = column.shape[0]
+        at = iota((n, nl), 1) - starts[k]
+        reached = (at >= iota((n, nl), 0)) & (at < n)
+        return jnp.sum(jnp.where(reached, column, 0), axis=0, keepdims=True)
     end = slice(nk - 1, nk)
     upto = (iota((ni, nl), 1) // nb) >= iota((ni, nl), 0)
 
@@ -208,6 +219,12 @@
         whole = jnp.broadcast_to(w[SUB - 1 : SUB], w.shape)
         for d in range(1, nb):
             w = w + jnp.where(block >= d, turn(whole, d, 1), 0)
+        return w
+
+    def stacked(values):
+        w = jnp.zeros((SUB, nl), I32)
+        for r, value in enumerate(values):
+            w = jnp.where(subs == r, value, w)
         return w
 
     def packed(column):
@@ -241,16 +258,17 @@
     ysv = ys[...]
     small = lane_scan(jnp.concatenate([ysv, hy[...], lines, total, q[0]], 0))[:, end]
     ends_of = jnp.broadcast_to(small[2 * ni : 2 * ni + SUB], (SUB, nl))
-    row = [
-        along(small[:ni]), ends_of[0:1], along(ysv[:, 0:1]),
-        jnp.broadcast_to(lines[0:1, 0:1], (1, nl)), along(small[ni : 2 * ni]),
-        ends_of[2:3], ends_of[1:2],
-    ]
-    rows = jnp.zeros((SUB, nl), I32)
-    for r, value in enumerate(row):
-        rows = jnp.where(subs == r, value, rows)
-    pk[0:SUB] = rows
-    pk[SUB:] = lines
+    whole, first_j, first_i = (ends_of[r : r + 1] for r in (0, 2, 1))
+    pk[0:SUB] = stacked([
+        along(small[:ni]), whole, along(ysv[:, 0:1]),
+        jnp.broadcast_to(lines[0:1, 0:1], (1, nl)), in_order(small[:ni], 2),
+        in_order(small[ni : 2 * ni], 3),
+    ])
+    pk[SUB:] = lines + stacked([
+        0, 0, 0, jnp.where(within(0) | within(2), whole, 0),
+        jnp.where(within(3), first_j, 0), jnp.where(within(1), first_i, 0),
+    ])
+
 
     outgoing = [
         (inside(X + dx, Y + dy), functools.partial(plane_copy, n))
@@ -281,7 +299,9 @@
     first = 2 * ni + SUB
     px[0:SUB] = j_scan(packed(small[first : first + nj]))
     px[SUB : 2 * SUB] = j_scan(packed(total[:, 0:1]))
-    px[2 * SUB :] = j_scan(packed(small[first + nj :]))
+    px[2 * SUB :] = stacked([
+        in_order(small[first : first + nj], 0), in_order(small[first + nj :], 1)
+    ])
     @pl.when(jnp.logical_not(first_y))
     def _():
         burst()
@@ -335,7 +355,12 @@
     for n in range(2, nx):
         xa = xa + pxin[n, 0:SUB]
     a0 = a0 + xa
-    xd = pxin[0, 2 * SUB :]
+    borders = pxin[0, 2 * SUB + 1 : 2 * SUB + 2]
+    for n in range(1, nx):
+        borders = borders + pxin[n, 2 * SUB : 2 * SUB + 1]
+    z_refs = (zs, zup, zss, zrs)
+    higher = ups("gz", *z_refs)
+    higher_rows = ups("gz", zr, zrin, rss, rrs)
     up_wait("gx", xs, xup, xss, xrs)
     down_wait("gx", q.at[0], xdn, 0)
     rxv = xup[0]
@@ -388,7 +413,14 @@
     def _():
         tails[...] = jnp.zeros_like(tails)
         by[...] = jnp.zeros_like(by)
+        zs[...] = a0
+        for here, copy in higher[-2:]:
+            send(here, copy)
         sweep_all()
+        for d in range(3, nz):
+            hear(d, Z == 0)
+        for here, copy in higher[:-2]:
+            send(here, copy)
 
     for n, (dx, dy) in enumerate(plane_to):
         @pl.when(inside(X - dx, Y - dy))
@@ -400,31 +432,25 @@
         return functools.reduce(jnp.add, found) if found else jnp.zeros((SUB, nk), I32)
 
     kinds = (
-        (lambda dx, dy: dx == 0 and dy > 0, 0), (lambda dx, dy: dx > 0 and dy > 0, 1),
-        (lambda dx, dy: dx == 0 and dy < 0, 4), (lambda dx, dy: dx > 0 and dy < 0, 5),
-        (lambda dx, dy: dx < 0, 6),
+        (lambda dx, dy: dx == 0 and dy > 0, 4), (lambda dx, dy: dx > 0 and dy > 0, SUB + 3),
+        (lambda dx, dy: dx == 0 and dy < 0, 5), (lambda dx, dy: dx > 0 and dy < 0, SUB + 4),
+        (lambda dx, dy: dx < 0, SUB + 5),
     )
-    low, corner, high, high_corner, before = (
-        gather(wanted, lambda n: pkin[n, 0:SUB])[r : r + 1] for wanted, r in kinds
-    )
-    y_low, y_high = low + corner, high + high_corner
-    front, back = xa + corner, xd + before
-    zs[0:SUB] = a0 + y_low
-    zs[SUB:] = jnp.where(
-        subs == 0, y_low,
-        jnp.where(
-            subs == 1, y_high,
-            jnp.where(
-                lanes < half, jnp.where(moved, pltpu.roll(front, 2, 0), front),
-                jnp.where(moved, pltpu.roll(back, 2, 0), back),
-            ),
-        ),
-    )
-    z_refs = (zs, zup, zss, zrs)
-    higher = ups("gz", *z_refs)
-    for d in range(2, nz):
-        hear(d, Z == 0)
-    for here, copy in higher:
+    for wanted, r in kinds:
+        at = r // SUB * SUB
+        borders = borders + gather(wanted, lambda n: pkin[n, at : at + SUB])[r - at : r - at + 1]
+    zr[...] = borders
+
+    @pl.when(jnp.logical_not(first_y))
+    def _():
+        low, corner = (gather(kinds[k][0], lambda n: pkin[n, 0:SUB]) for k in (0, 1))
+        zs[...] = a0 + (low[0:1] + corner[1:2])
+        for d in range(2, nz):
+            hear(d, Z == 0)
+        for here, copy in higher:
+            send(here, copy)
+
+    for here, copy in higher_rows:
         send(here, copy)
 
     up_wait("gy", ys, yup, yss, yrs)
@@ -432,14 +458,9 @@
     ryv = yup[0]
     for d in range(1, ny - 1):
         ryv = ryv + yup[d]
-    tail = lambda n: pkin[n, SUB:]
-    rytv = jnp.where(
-        sk == 0, gather(kinds[1][0], tail),
-        jnp.where(
-            sk == 1, gather(kinds[4][0], tail),
-            jnp.where(sk == 2, gather(kinds[3][0], tail), 0),
-        ),
-    )
+    rytv = stacked([
+        gather(kinds[k][0], lambda n: pkin[n, SUB:])[r : r + 1] for r, k in enumerate((1, 4, 3))
+    ])
     ly = lane_scan(jnp.concatenate([ryv, ydn[...], rytv], 0))
     lyl, lyh, lyt = ly[:ni], ly[ni : 2 * ni], ly[2 * ni :]
     rows_i = iota((ni, nk), 0)
@@ -463,31 +484,33 @@
 
     down_wait("gz", ds, zdn, 2)
     up_wait("gz", *z_refs)
+    up_wait("gz", zr, zrin, rss, rrs)
     beyond = zdn[...]
     for n, (dx, dy) in enumerate(level_to):
         r = 2 if dx == 0 else 3
         beyond = beyond + (dgin[n, r : r + 1, :] if dy else dgin[n])
-    carry = zup[0]
+    D, borders = zup[0], zrin[0]
     for d in range(1, nz - 1):
-        carry = carry + zup[d]
-    D, edges = carry[0:SUB], carry[SUB:]
-    y_low = jnp.broadcast_to(edges[0:1], D.shape)
-    y_high = jnp.where(last_y, 0, jnp.broadcast_to(edges[1:2], D.shape))
-    lifted = pltpu.roll(edges, SUB - 2, 0)
+        D, borders = D + zup[d], borders + zrin[d]
+    borders = jnp.broadcast_to(borders, D.shape)
+
+    def pick(index):
+        return jnp.take_along_axis(borders, index, 1, mode="promise_in_bounds")
+
+    front, back = pick(block * SUB + subs), pick(nj + block * SUB + subs)
     prior, after = pltpu.roll(D, 1, 0), pltpu.roll(D, SUB - 1, 0)
 
     def finals(by):
         at = lax.rem(lanes + (nl - by), nl)
         moved_to = lambda w, d: turn(w, d + by, 1)
         here = moved_to(D, 0)
-        front = jnp.where(subs < 2, moved_to(lifted, nl - nb), moved_to(edges, 0))
-        back = jnp.where(subs < 2, moved_to(lifted, 0), moved_to(edges, nb))
+        y_low, y_high = (pick(starts[k] + at // nb) for k in (2, 3))
         down_i = jnp.where(at < nb, front, moved_to(D, nb))
         edge_i = jnp.where(last_x, 0, here + back)
         up_i = jnp.where(at >= nl - nb, edge_i, moved_to(D, nl - nb))
-        edge_j = jnp.where(block == 0, moved_to(y_low, 0), moved_to(prior, 1))
+        edge_j = jnp.where(block == 0, y_low, moved_to(prior, 1))
         down_j = jnp.where(subs == 0, edge_j, moved_to(prior, 0))
-        edge_j = jnp.where(last_y, 0, here + moved_to(y_high, 0))
+        edge_j = jnp.where(last_y, 0, here + y_high)
         edge_j = jnp.where(block == nb - 1, edge_j, moved_to(after, nl - 1))
         up_j = jnp.where(subs == SUB - 1, edge_j, moved_to(after, 0))
         E = 8 * here + (down_i + up_i) + (down_j + up_j)
@@ -498,7 +521,7 @@
     eh_ref[0:SUB] = jnp.where(lanes < half, E, EH_half)
     eh_ref[SUB : 2 * SUB] = jnp.where(lanes < half, E_half, EH)
 
-    finish_sends(higher)
+    finish_sends([*higher, *higher_rows])
 
 
 def messages(nx, ny):
@@ -557,13 +580,14 @@
             vm(ni, nk), vm(ny - 1, ni, nk), vm(ni, nk), vm(ni, nk),
             vm(2 * SUB, nl), vm(np_, 2 * SUB, nl), vm(3 * SUB, nl), vm(nx, 3 * SUB, nl),
             vm(ng, SUB, nl),
-            vm(2 * SUB, nl), vm(nz - 1, 2 * SUB, nl), vm(SUB, nl), vm(SUB, nl),
+            vm(SUB, nl), vm(nz - 1, SUB, nl), vm(1, nl), vm(nz - 1, 1, nl),
+            vm(SUB, nl), vm(SUB, nl),
             vm(nj, nk), vm(nj, nk), vm(ni, nk), vm(ni, nk), vm(SUB, nk),
         ]
         semaphores = [
             pltpu.SemaphoreType.DMA,
             dma(nx - 1), dma(nx - 1), dma(ny - 1), dma(ny - 1),
-            dma(np_), dma(np_), dma(nx), dma(nx), dma(ng), dma(ng), dma(nz - 1), dma(nz - 1),
+            dma(np_), dma(np_), dma(nx), dma(nx), dma(ng), dma(ng), *[dma(nz - 1)] * 4,
             dma(3), dma(3),
             pltpu.SemaphoreType.REGULAR((max(nz - 2, 1),)),
         ]

time: 9.62 us -> 9.43 us (0.980)
  Pallas kernels: 8.8 us -> 8.61 us
    pallas_call x1, Pallas kernels: 7.78 us -> 7.59 us  [on_device(): pl.pallas_call(scoped, out_shape=(jax.ShapeDtypeStruct((ni, nj, nk), I32)...]
where the time goes in v4:
time: 9.43 us; the launch traced here: 9.26 us
  Pallas kernels  8.61 us (91%)
  between operations  0.65 us (7%)
    pallas_call x1, Pallas kernels, on_device(): pl.pallas_call(scoped, out_shape=(jax.ShapeDtypeStruct((ni, nj, nk), I32)...  7.59 us
    pallas_call x1, Pallas kernels, on_device(): pl.pallas_call(finish, out_shape=jax.ShapeDtypeStruct((ni, nj, nk), F32),...  1.02 us

profile of v4, /device:TPU:0, one launch (start us, length us, event | category | flops | bytes accessed | tf_op | source)
XLA Modules:
  0.0 9.3 jit_solution(17139644510704129660)
XLA Ops:
  0.7 7.6 %exchange.1 = (s32[32,32,128]{2,1,0:T(8,128)S(1)}, s32[16,128]{1,0:T(8,128)S(1)}) custom-call(s32[32,32,128]{2,1,0:T(8,128)} %refs_0_.1), custom_call_target="tpu_custom_call" | custom-call | tf_op jit(solution)/shard_map/exchange/pallas_call | solution.py:604
  8.2 1.0 %finish.1 = f32[32,32,128]{2,1,0:T(8,128)} custom-call(f32[1]{0:T(128)S(6)} %copy.3.step_ref, s32[32,32,128]{2,1,0:T(8,128)S(1)} %get-tuple-element.7.v_ref, s32[16,128]{1,0:T(8,128)S(1)} %get-tuple-element.8.eh_ref), custom_call_target="tpu_custom_call" | custom-call | tf_op jit(solution)/shard_map/finish/pallas_call | solution.py:618

commit v5 on v4

--- a/solution.py
+++ b/solution.py
@@ -87,15 +87,20 @@
         ok = (x >= 0) & (x < nx) & (y >= 0) & (y < ny)
         return ok if isinstance(z, int) else ok & (z >= 0) & (z < nz)
 
-    for dx in range(nx):
-        for dy in range(ny):
-            if dx or dy:
-                greet({"gx": lax.rem(X + dx, nx), "gy": lax.rem(Y + dy, ny)}, barrier)
+    def greet_plane(dx, dy):
+        greet({"gx": lax.rem(X + dx, nx), "gy": lax.rem(Y + dy, ny)}, barrier)
+
+    for dy in range(1, ny):
+        greet_plane(0, dy)
     first_y = Y == 0
     for d in (-2, -1, 1):
         @pl.when((Z + d >= 0) & (Z + d < nz) & (first_y if d == -2 else True))
         def _(d=d):
             greet({"gz": Z + d}, barrier)
+
+    for dx in range(1, nx):
+        for dy in range(ny):
+            greet_plane(dx, dy)
 
     for dx, dy in level_to:
         @pl.when(inside(X - dx, Y - dy, Z + 1))
@@ -615,12 +620,15 @@
             ),
             name="exchange",
         )(pltpu.with_memory_space_constraint(quant_codes, pltpu.HBM))
+        def finish_scoped(*refs):
+            pl.run_scoped(functools.partial(finish, *refs), dma(8))
+
         return pl.pallas_call(
-            finish,
+            finish_scoped,
             out_shape=jax.ShapeDtypeStruct((ni, nj, nk), F32),
             in_specs=[pl.BlockSpec(memory_space=pltpu.SMEM), vmem, vmem],
             out_specs=any_space,
-            scratch_shapes=[pltpu.VMEM((ni, nj, nk), F32), dma(8)],
+            scratch_shapes=[pltpu.VMEM((ni, nj, nk), F32)],
             compiler_params=pltpu.CompilerParams(vmem_limit_bytes=16 * 2**20),
             name="finish",
         )(error_step, v, eh)

time: 9.43 us -> 9.32 us (0.988)
  Pallas kernels: 8.61 us -> 8.5 us
where the time goes in v5:
time: 9.32 us; the launch traced here: 9.16 us
  Pallas kernels  8.5 us (91%)
  between operations  0.65 us (7%)
    pallas_call x1, Pallas kernels, on_device(): pl.pallas_call(scoped, out_shape=(jax.ShapeDtypeStruct((ni, nj, nk), I32)...  7.55 us
    pallas_call x1, Pallas kernels, on_device(): pl.pallas_call(finish_scoped, out_shape=jax.ShapeDtypeStruct((ni, nj, nk)...  0.95 us

profile of v5, /device:TPU:0, one launch (start us, length us, event | category | flops | bytes accessed | tf_op | source)
XLA Modules:
  0.0 9.2 jit_solution(3464596394612666693)
XLA Ops:
  0.7 7.6 %exchange.1 = (s32[32,32,128]{2,1,0:T(8,128)S(1)}, s32[16,128]{1,0:T(8,128)S(1)}) custom-call(s32[32,32,128]{2,1,0:T(8,128)} %refs_0_.2), custom_call_target="tpu_custom_call" | custom-call | tf_op jit(solution)/shard_map/exchange/pallas_call | solution.py:609
  8.2 1.0 %finish.1 = f32[32,32,128]{2,1,0:T(8,128)} custom-call(f32[1]{0:T(128)S(6)} %copy.3.refs_0_, s32[32,32,128]{2,1,0:T(8,128)S(1)} %get-tuple-element.7.refs_1_, s32[16,128]{1,0:T(8,128)S(1)} %get-tuple-element.8.refs_2_), custom_call_target="tpu_custom_call" | custom-call | tf_op jit(solution)/shard_map/finish/pallas_call | solution.py:626

commit v6 on v5

--- a/solution.py
+++ b/solution.py
@@ -366,6 +366,17 @@
     z_refs = (zs, zup, zss, zrs)
     higher = ups("gz", *z_refs)
     higher_rows = ups("gz", zr, zrin, rss, rrs)
+    zs[...] = a0
+    hear(2, Z == 0)
+    for n, (here, copy) in enumerate(higher):
+        send(here & (Z > 0) if n < len(higher) - 2 else here, copy)
+
+    def send_far():
+        for d in range(3, nz):
+            hear(d, Z == 0)
+        for here, copy in higher[:-2]:
+            send(here & (Z == 0), copy)
+
     up_wait("gx", xs, xup, xss, xrs)
     down_wait("gx", q.at[0], xdn, 0)
     rxv = xup[0]
@@ -418,14 +429,8 @@
     def _():
         tails[...] = jnp.zeros_like(tails)
         by[...] = jnp.zeros_like(by)
-        zs[...] = a0
-        for here, copy in higher[-2:]:
-            send(here, copy)
         sweep_all()
-        for d in range(3, nz):
-            hear(d, Z == 0)
-        for here, copy in higher[:-2]:
-            send(here, copy)
+        send_far()
 
     for n, (dx, dy) in enumerate(plane_to):
         @pl.when(inside(X - dx, Y - dy))
@@ -448,12 +453,7 @@
 
     @pl.when(jnp.logical_not(first_y))
     def _():
-        low, corner = (gather(kinds[k][0], lambda n: pkin[n, 0:SUB]) for k in (0, 1))
-        zs[...] = a0 + (low[0:1] + corner[1:2])
-        for d in range(2, nz):
-            hear(d, Z == 0)
-        for here, copy in higher:
-            send(here, copy)
+        send_far()
 
     for here, copy in higher_rows:
         send(here, copy)
@@ -489,37 +489,52 @@
 
     down_wait("gz", ds, zdn, 2)
     up_wait("gz", *z_refs)
-    up_wait("gz", zr, zrin, rss, rrs)
     beyond = zdn[...]
     for n, (dx, dy) in enumerate(level_to):
         r = 2 if dx == 0 else 3
         beyond = beyond + (dgin[n, r : r + 1, :] if dy else dgin[n])
-    D, borders = zup[0], zrin[0]
+    D = zup[0]
     for d in range(1, nz - 1):
-        D, borders = D + zup[d], borders + zrin[d]
+        D = D + zup[d]
+    prior, after = pltpu.roll(D, 1, 0), pltpu.roll(D, SUB - 1, 0)
+
+    def raw(by):
+        moved_to = lambda w, d: turn(w, d + by, 1)
+        here = moved_to(D, 0)
+        down_j = jnp.where(
+            subs == 0, jnp.where(block == 0, 0, moved_to(prior, 1)), moved_to(prior, 0)
+        )
+        edge_j = jnp.where(block == nb - 1, here, moved_to(after, nl - 1))
+        up_j = jnp.where(subs == SUB - 1, edge_j, moved_to(after, 0))
+        return here, moved_to(D, nb), moved_to(D, nl - nb), down_j, up_j, moved_to(beyond, 0)
+
+    raws = raw(0), raw(half)
+    up_wait("gz", zr, zrin, rss, rrs)
+    borders = zrin[0]
+    for d in range(1, nz - 1):
+        borders = borders + zrin[d]
     borders = jnp.broadcast_to(borders, D.shape)
 
     def pick(index):
         return jnp.take_along_axis(borders, index, 1, mode="promise_in_bounds")
 
     front, back = pick(block * SUB + subs), pick(nj + block * SUB + subs)
-    prior, after = pltpu.roll(D, 1, 0), pltpu.roll(D, SUB - 1, 0)
+    corner_j = (subs == SUB - 1) & (block == nb - 1)
 
     def finals(by):
+        here, down_i, up_i, down_j, up_j, past = raws[by // half]
         at = lax.rem(lanes + (nl - by), nl)
-        moved_to = lambda w, d: turn(w, d + by, 1)
-        here = moved_to(D, 0)
-        y_low, y_high = (pick(starts[k] + at // nb) for k in (2, 3))
-        down_i = jnp.where(at < nb, front, moved_to(D, nb))
+        g = at // nb
+        low = pick(starts[2] + g)
+        here = here + low
+        down_i = jnp.where(at < nb, front, down_i + pick(starts[2] + jnp.maximum(g - 1, 0)))
         edge_i = jnp.where(last_x, 0, here + back)
-        up_i = jnp.where(at >= nl - nb, edge_i, moved_to(D, nl - nb))
-        edge_j = jnp.where(block == 0, y_low, moved_to(prior, 1))
-        down_j = jnp.where(subs == 0, edge_j, moved_to(prior, 0))
-        edge_j = jnp.where(last_y, 0, here + y_high)
-        edge_j = jnp.where(block == nb - 1, edge_j, moved_to(after, nl - 1))
-        up_j = jnp.where(subs == SUB - 1, edge_j, moved_to(after, 0))
-        E = 8 * here + (down_i + up_i) + (down_j + up_j)
-        return E, E + jnp.where(last_z, -here, moved_to(beyond, 0))
+        next_low = pick(starts[2] + jnp.minimum(g + 1, ni - 1))
+        up_i = jnp.where(at >= nl - nb, edge_i, up_i + next_low)
+        edge_j = jnp.where(last_y, 0, here + pick(starts[3] + g))
+        up_j = jnp.where(corner_j, edge_j, up_j + low)
+        E = 8 * here + (down_i + up_i) + (down_j + low + up_j)
+        return E, E + jnp.where(last_z, -here, past)
 
     E, EH = finals(0)
     E_half, EH_half = finals(half)

time: 9.32 us -> 9.32 us (level)
  no operation moved by 1% of the time
where the time goes in v6:
time: 9.32 us; the launch traced here: 9.16 us
  Pallas kernels  8.5 us (91%)
  between operations  0.66 us (7%)
    pallas_call x1, Pallas kernels, on_device(): pl.pallas_call(scoped, out_shape=(jax.ShapeDtypeStruct((ni, nj, nk), I32)...  7.55 us
    pallas_call x1, Pallas kernels, on_device(): pl.pallas_call(finish_scoped, out_shape=jax.ShapeDtypeStruct((ni, nj, nk)...  0.95 us

profile of v6, /device:TPU:0, one launch (start us, length us, event | category | flops | bytes accessed | tf_op | source)
XLA Modules:
  0.0 9.2 jit_solution(9835509060993863918)
XLA Ops:
  0.7 7.5 %exchange.1 = (s32[32,32,128]{2,1,0:T(8,128)S(1)}, s32[16,128]{1,0:T(8,128)S(1)}) custom-call(s32[32,32,128]{2,1,0:T(8,128)} %refs_0_.2), custom_call_target="tpu_custom_call" | custom-call | tf_op jit(solution)/shard_map/exchange/pallas_call | solution.py:624
  8.2 1.0 %finish.1 = f32[32,32,128]{2,1,0:T(8,128)} custom-call(f32[1]{0:T(128)S(6)} %copy.3.refs_0_, s32[32,32,128]{2,1,0:T(8,128)S(1)} %get-tuple-element.7.refs_1_, s32[16,128]{1,0:T(8,128)S(1)} %get-tuple-element.8.refs_2_), custom_call_target="tpu_custom_call" | custom-call | tf_op jit(solution)/shard_map/finish/pallas_call | solution.py:641

commit v7 on v6

--- a/solution.py
+++ b/solution.py
@@ -61,7 +61,7 @@
 
 def exchange(
     mesh_sizes, q_hbm, v_ref, eh_ref,
-    q, scan, xs, xup, xdn, ys, yup, hy, ydn, pk, pkin, px, pxin, dgin,
+    q, scan, xs, xup, xdn, ys, yup, hy, ydn, pr, prin, pk, pkin, px, pxin, dgin,
     zs, zup, zr, zrin, ds, zdn, ax, hxc, by, hyc, tails,
     load_sem, xss, xrs, yss, yrs, pss, prs, ass, ars, gss, grs, zss, zrs, rss, rrs, dss, drs, ready,
 ):
@@ -123,8 +123,8 @@
         clear(jnp.logical_not(inside(X - dx, Y)), pxin.at[n])
     for n, (dx, dy) in enumerate(level_to):
         clear(jnp.logical_not(inside(X - dx, Y - dy, Z + 1)), dgin.at[n])
-    for axis, slots, beyond in (("gx", xup, xdn), ("gy", yup, ydn), ("gz", zup, zdn), ("gz", zrin, None)):
-        for d in range(1, size[axis]):
+    for axis, slots, beyond in (("gx", xup, xdn), ("gy", yup, ydn), ("gz", zup, zdn), ("gz", zrin, None), ("gy", None, prin)):
+        for d in range(1, size[axis]) if slots is not None else ():
             clear(place[axis] < d, slots.at[d - 1])
         if beyond is not None:
             clear(place[axis] == size[axis] - 1, beyond)
@@ -267,15 +267,15 @@
     pk[0:SUB] = stacked([
         along(small[:ni]), whole, along(ysv[:, 0:1]),
         jnp.broadcast_to(lines[0:1, 0:1], (1, nl)), in_order(small[:ni], 2),
-        in_order(small[ni : 2 * ni], 3),
     ])
+    pr[...] = in_order(small[ni : 2 * ni], 3)
     pk[SUB:] = lines + stacked([
         0, 0, 0, jnp.where(within(0) | within(2), whole, 0),
         jnp.where(within(3), first_j, 0), jnp.where(within(1), first_i, 0),
     ])
 
 
-    outgoing = [
+    outgoing = downs("gy", pr, prin, 3) + [
         (inside(X + dx, Y + dy), functools.partial(plane_copy, n))
         for n, (dx, dy) in enumerate(plane_to)
     ] + [
@@ -437,13 +437,16 @@
         def _(n=n):
             plane_copy(n).wait_recv()
 
+    down_wait("gy", pr, prin, 3)
+    borders = borders + prin[...]
+
     def gather(wanted, slots):
         found = [slots(n) for n, m in enumerate(plane_to) if wanted(*m)]
         return functools.reduce(jnp.add, found) if found else jnp.zeros((SUB, nk), I32)
 
     kinds = (
         (lambda dx, dy: dx == 0 and dy > 0, 4), (lambda dx, dy: dx > 0 and dy > 0, SUB + 3),
-        (lambda dx, dy: dx == 0 and dy < 0, 5), (lambda dx, dy: dx > 0 and dy < 0, SUB + 4),
+        (lambda dx, dy: dx > 0 and dy < 0, SUB + 4),
         (lambda dx, dy: dx < 0, SUB + 5),
     )
     for wanted, r in kinds:
@@ -464,7 +467,7 @@
     for d in range(1, ny - 1):
         ryv = ryv + yup[d]
     rytv = stacked([
-        gather(kinds[k][0], lambda n: pkin[n, SUB:])[r : r + 1] for r, k in enumerate((1, 4, 3))
+        gather(kinds[k][0], lambda n: pkin[n, SUB:])[r : r + 1] for r, k in enumerate((1, 3, 2))
     ])
     ly = lane_scan(jnp.concatenate([ryv, ydn[...], rytv], 0))
     lyl, lyh, lyt = ly[:ni], ly[ni : 2 * ni], ly[2 * ni :]
@@ -482,17 +485,7 @@
         v_ref[i, nj - SUB : nj, :] += jnp.where(last_y, 0, beyond_j)
 
     finish_sends([*outgoing, (below, down_ds)])
-    for n, (dx, dy) in enumerate(level_to):
-        @pl.when(inside(X - dx, Y - dy, Z + 1))
-        def _(n=n):
-            level_copy(n).wait_recv()
-
-    down_wait("gz", ds, zdn, 2)
     up_wait("gz", *z_refs)
-    beyond = zdn[...]
-    for n, (dx, dy) in enumerate(level_to):
-        r = 2 if dx == 0 else 3
-        beyond = beyond + (dgin[n, r : r + 1, :] if dy else dgin[n])
     D = zup[0]
     for d in range(1, nz - 1):
         D = D + zup[d]
@@ -506,7 +499,7 @@
         )
         edge_j = jnp.where(block == nb - 1, here, moved_to(after, nl - 1))
         up_j = jnp.where(subs == SUB - 1, edge_j, moved_to(after, 0))
-        return here, moved_to(D, nb), moved_to(D, nl - nb), down_j, up_j, moved_to(beyond, 0)
+        return here, moved_to(D, nb), moved_to(D, nl - nb), down_j, up_j
 
     raws = raw(0), raw(half)
     up_wait("gz", zr, zrin, rss, rrs)
@@ -522,7 +515,7 @@
     corner_j = (subs == SUB - 1) & (block == nb - 1)
 
     def finals(by):
-        here, down_i, up_i, down_j, up_j, past = raws[by // half]
+        here, down_i, up_i, down_j, up_j = raws[by // half]
         at = lax.rem(lanes + (nl - by), nl)
         g = at // nb
         low = pick(starts[2] + g)
@@ -534,10 +527,21 @@
         edge_j = jnp.where(last_y, 0, here + pick(starts[3] + g))
         up_j = jnp.where(corner_j, edge_j, up_j + low)
         E = 8 * here + (down_i + up_i) + (down_j + low + up_j)
-        return E, E + jnp.where(last_z, -here, past)
-
-    E, EH = finals(0)
-    E_half, EH_half = finals(half)
+        return E, here
+
+    (E, here), (E_half, here_half) = finals(0), finals(half)
+    for n, (dx, dy) in enumerate(level_to):
+        @pl.when(inside(X - dx, Y - dy, Z + 1))
+        def _(n=n):
+            level_copy(n).wait_recv()
+
+    down_wait("gz", ds, zdn, 2)
+    beyond = zdn[...]
+    for n, (dx, dy) in enumerate(level_to):
+        r = 2 if dx == 0 else 3
+        beyond = beyond + (dgin[n, r : r + 1, :] if dy else dgin[n])
+    EH = E + jnp.where(last_z, -here, beyond)
+    EH_half = E_half + jnp.where(last_z, -here_half, turn(beyond, half, 1))
     eh_ref[0:SUB] = jnp.where(lanes < half, E, EH_half)
     eh_ref[SUB : 2 * SUB] = jnp.where(lanes < half, E_half, EH)
 
@@ -545,7 +549,7 @@
 
 
 def messages(nx, ny):
-    plane = [(dx, -1) for dx in range(nx)] + [
+    plane = [(dx, -1) for dx in range(1, nx)] + [
         (dx, dy) for dy in range(ny - 1, 0, -1) for dx in range(-1, nx)
     ]
     level = [(dx, dy) for dy in range(ny - 1, -1, -1) for dx in range(nx) if dx or dy]
@@ -598,7 +602,7 @@
             vm(ni, nj, nk), vm(ni, nj, nk),
             vm(nj, nk), vm(nx - 1, nj, nk), vm(nj, nk),
             vm(ni, nk), vm(ny - 1, ni, nk), vm(ni, nk), vm(ni, nk),
-            vm(2 * SUB, nl), vm(np_, 2 * SUB, nl), vm(3 * SUB, nl), vm(nx, 3 * SUB, nl),
+            vm(1, nl), vm(1, nl), vm(2 * SUB, nl), vm(np_, 2 * SUB, nl), vm(3 * SUB, nl), vm(nx, 3 * SUB, nl),
             vm(ng, SUB, nl),
             vm(SUB, nl), vm(nz - 1, SUB, nl), vm(1, nl), vm(nz - 1, 1, nl),
             vm(SUB, nl), vm(SUB, nl),
@@ -608,7 +612,7 @@
             pltpu.SemaphoreType.DMA,
             dma(nx - 1), dma(nx - 1), dma(ny - 1), dma(ny - 1),
             dma(np_), dma(np_), dma(nx), dma(nx), dma(ng), dma(ng), *[dma(nz - 1)] * 4,
-            dma(3), dma(3),
+            dma(4), dma(4),
             pltpu.SemaphoreType.REGULAR((max(nz - 2, 1),)),
         ]
 

time: 9.32 us -> 9.28 us (level)
  no operation moved by 1% of the time
where the time goes in v7:
time: 9.28 us; the launch traced here: 9.12 us
  Pallas kernels  8.46 us (91%)
  between operations  0.65 us (7%)
    pallas_call x1, Pallas kernels, on_device(): pl.pallas_call(scoped, out_shape=(jax.ShapeDtypeStruct((ni, nj, nk), I32)...  7.51 us
    pallas_call x1, Pallas kernels, on_device(): pl.pallas_call(finish_scoped, out_shape=jax.ShapeDtypeStruct((ni, nj, nk)...  0.95 us

profile of v7, /device:TPU:0, one launch (start us, length us, event | category | flops | bytes accessed | tf_op | source)
XLA Modules:
  0.0 9.1 jit_solution(3788803043207255609)
XLA Ops:
  0.7 7.5 %exchange.1 = (s32[32,32,128]{2,1,0:T(8,128)S(1)}, s32[16,128]{1,0:T(8,128)S(1)}) custom-call(s32[32,32,128]{2,1,0:T(8,128)} %refs_0_.2), custom_call_target="tpu_custom_call" | custom-call | tf_op jit(solution)/shard_map/exchange/pallas_call | solution.py:628
  8.2 1.0 %finish.1 = f32[32,32,128]{2,1,0:T(8,128)} custom-call(f32[1]{0:T(128)S(6)} %copy.3.refs_0_, s32[32,32,128]{2,1,0:T(8,128)S(1)} %get-tuple-element.7.refs_1_, s32[16,128]{1,0:T(8,128)S(1)} %get-tuple-element.8.refs_2_), custom_call_target="tpu_custom_call" | custom-call | tf_op jit(solution)/shard_map/finish/pallas_call | solution.py:645
